TPU v7x, 32 devices: a whole 2x2x4 slice. The times are simulated.
32 devices in a mesh: region: 16 (over z, y, x), member: 2 (over core).
Axes of the slice: x: 2, y: 2, z: 4, core: 2. Of those that a mesh axis runs over, the one named last changes fastest.
Arguments:
- perturbations: bfloat16 [80, 2, 64, 2048], P('member', None, None, 'region'), may hold values from -0.65625 to 0.65625
- control: float32 [80, 64, 2048], P('member', None, 'region'), may hold values from -6 to 6
- vertical_loc: bfloat16 [64, 64], replicated, may hold values from -0.75 to 0.75
- block_kernels: bfloat16 [4, 128, 128], replicated, may hold values from -0.3125 to 0.3125
- loc_pattern: int32 [16, 3], replicated, may hold values from 0 to 3
- obs_region: int32 [16384, 1], P('region'), may hold values from 0 to 15; in each aligned block of 512 rows (0 to 511, 512 to 1023, ...) at most 64 rows name the same one
- obs_slot: int32 [16384], P('region'), may hold values from 0 to 1
- obs_cell: int32 [16384], P('region'), may hold values from 0 to 127
- innovations: float32 [64, 16384], P(None, 'region'), may hold values from -12 to 12
- obs_weight: float32 [128, 128, 128], P('region'), may hold values from -0.0375 to 2, as said below
Outputs:
- analysis: float32 [80, 64, 2048], P('member', None, 'region')
Inputs may be any that keep to these rules, and one draw needn't show every extreme that they name: `obs_region`: in each aligned block of 512 rows, no region is named by more than 64 rows. `obs_weight`: each tile is symmetric, and in each row the diagonal entry exceeds the sum of the magnitudes of the other entries.
All inputs are finite; a program needn't handle non-finite values.
Results may differ from a plain program's by a relative error of at most 0.013.
Values may be sent and summed in bfloat16 or wider, within the bound.
No kernel may reach another device: no remote copies, remote signals or barrier semaphores. Data moves between devices by JAX's collectives and lax.ppermute only.
A program may use at most 64 MiB of HBM per device.

v0:
```python
import functools

import jax
import jax.numpy as jnp
from jax import lax
from jax.experimental import pallas as pl
from jax.experimental.pallas import tpu as pltpu
from jax.sharding import PartitionSpec as P


SLOTS = 2
TILE = 128
CELLS = 128
CODES = SLOTS * CELLS
F32 = jnp.float32
BF16 = jnp.bfloat16
HALO_CHUNKS = 5


def near_of(r):
    return r ^ 1


def far_of(r, regions):
    other = r - 1 if r % 2 == 0 else r + 1
    return other if 0 <= other < regions else None


def side(r, t, regions):
    return (r, near_of(r), far_of(r, regions))[t]


def dot(a, b, dims=((1,), (0,)), precision=None):
    return lax.dot_general(a, b, (dims, ((), ())), precision=precision, preferred_element_type=F32)


def halo(chunks):
    regions = lax.axis_size("region")
    pairs = [(r, r ^ 1) for r in range(regions)]
    onward = [(r, r + 2 if r % 2 == 0 else r - 2) for r in range(regions)]
    onward = [(s, d) for s, d in onward if 0 <= d < regions]
    near = [lax.ppermute(c, "region", pairs) for c in chunks]
    far = [lax.ppermute(c, "region", onward) for c in near]
    return near, far


def call(kernel, out_shape, args, scratch=(), limit=16, scalars=()):
    vmem = pl.BlockSpec(memory_space=pltpu.VMEM)
    return pl.pallas_call(
        kernel,
        out_shape=out_shape,
        in_specs=[pl.BlockSpec(memory_space=pltpu.SMEM)] * len(scalars) + [vmem] * len(args),
        out_specs=jax.tree.map(lambda _: vmem, out_shape),
        scratch_shapes=list(scratch),
        compiler_params=pltpu.CompilerParams(vmem_limit_bytes=limit << 20),
    )(*scalars, *[pltpu.with_memory_space_constraint(a, pltpu.VMEM) for a in args])


def group_size(members):
    return 4 if members % 4 == 0 else 2 if members % 2 == 0 else 1


def shape(dims, dtype):
    return pltpu.VMEM(dims, dtype)


def block_diagonal(matrix, copies, transposed):
    size = matrix.shape[0]
    total = copies * size
    row = lax.broadcasted_iota(jnp.int32, (total, size), 0)
    place = (row % size == lax.broadcasted_iota(jnp.int32, (total, size), 1)).astype(BF16)
    tall = dot(place, matrix, ((1,), (1 if transposed else 0,))).astype(BF16)
    wide = dot(tall, place, ((1,), (1,)))
    same = (
        lax.broadcasted_iota(jnp.int32, (total, total), 0) // size
        == lax.broadcasted_iota(jnp.int32, (total, total), 1) // size
    )
    return jnp.where(same, wide, 0.0).astype(BF16)


def own_kernel(group, pattern, start, pert, kernels, vloc, inc, lifted, tables, vert, vert_t, acc):
    count, lev, _ = start.shape
    rows = group * lev
    acc[...] = jnp.zeros_like(acc)
    vert[...] = block_diagonal(vloc[...], group, False)
    vert_t[...] = block_diagonal(vloc[...], group, True)
    region = lax.axis_index("region")
    even = region % 2 == 0
    up = pattern[jnp.minimum(region + 1, pattern.shape[0] - 1), 0]
    down = pattern[jnp.maximum(region - 1, 0), 2]
    picks = (pattern[region, 1], jnp.where(even, up, down), jnp.where(even, down, up))
    for t in range(3):
        tables[:, t * CELLS : (t + 1) * CELLS] = kernels[picks[t]]

    def step(g, _):
        at = pl.ds(g * group, group)
        mixed = dot(vert[...], start[at].reshape(rows, CELLS).astype(BF16)).astype(BF16)
        lifted[at] = mixed.reshape(group, lev, CELLS)
        local = dot(mixed, tables[:, :CELLS])
        for s in range(SLOTS):
            total = acc[s]
            for j in range(group):
                total += pert[g * group + j, s].astype(F32) * local[j * lev : (j + 1) * lev]
            acc[s] = total
        return 0

    lax.fori_loop(0, count // group, step, 0, unroll=2)
    inc[...] = acc[...]


def own_forward(pattern, start, pert, kernels, vloc, group):
    _, lev, _ = start.shape
    field = (SLOTS, lev, CELLS)
    square = shape((group * lev, group * lev), BF16)
    out = (shape(field, F32), shape(start.shape, BF16), shape((CELLS, 3 * CELLS), BF16), square, square)
    return call(
        functools.partial(own_kernel, group),
        out,
        [start, pert, kernels, vloc],
        [pltpu.VMEM(field, F32)],
        scalars=[pattern],
    )


def part_sum(n, group, t, chunks, lifted, tables, acc, full):
    lev = lifted.shape[1]
    rows = group * lev
    acc[...] = jnp.zeros_like(acc)
    first = 0
    for ch in range(n):
        size = chunks[ch].shape[0]

        def step(g, _, ch=ch, first=first):
            at = pl.ds(first + g * group, group)
            local = dot(lifted[at].reshape(rows, CELLS), tables[:, t * CELLS : (t + 1) * CELLS])
            values = chunks[ch][pl.ds(g * group, group)]
            full[at] = values
            for s in range(SLOTS):
                total = acc[s]
                for j in range(group):
                    total += values[j, s].astype(F32) * local[j * lev : (j + 1) * lev]
                acc[s] = total
            return 0

        lax.fori_loop(0, size // group, step, 0, unroll=size // group)
        first += size


def near_kernel(n, group, *refs):
    chunks = refs[:n]
    lifted, tables, inc, full, acc = refs[n:]
    part_sum(n, group, 1, chunks, lifted, tables, acc, full)
    inc[...] = acc[...]


def joined(chunks):
    return shape((sum(c.shape[0] for c in chunks),) + chunks[0].shape[1:], chunks[0].dtype)


def near_forward(chunks, lifted, tables, group):
    field = (SLOTS, lifted.shape[1], CELLS)
    return call(
        functools.partial(near_kernel, len(chunks), group),
        (shape(field, F32), joined(chunks)),
        [*chunks, lifted, tables],
        [pltpu.VMEM(field, F32)],
    )


def far_kernel(n, group, *refs):
    chunks = refs[:n]
    own, near, lifted, tables, inc, half, full, acc = refs[n:]
    part_sum(n, group, 2, chunks, lifted, tables, acc, full)
    for t, part in enumerate((own, near, acc)):
        inc[t] = part[...]
        half[t] = part[...].astype(BF16)


def far_forward(chunks, own, near, lifted, tables, group):
    field = (SLOTS, lifted.shape[1], CELLS)
    return call(
        functools.partial(far_kernel, len(chunks), group),
        (shape((3,) + field, F32), shape((3,) + field, BF16), joined(chunks)),
        [*chunks, own, near, lifted, tables],
        [pltpu.VMEM(field, F32)],
    )


def columns(row, width):
    return jnp.broadcast_to(row.astype(F32), (width, row.shape[1])).T.astype(jnp.int32)


def lane_choice(column, start, width):
    lanes = lax.broadcasted_iota(jnp.int32, column.shape, 1)
    blocks = [jnp.where(column == lanes + (start + b), 1.0, 0.0).astype(BF16) for b in range(0, width, column.shape[1])]
    return blocks[0] if len(blocks) == 1 else jnp.concatenate(blocks, axis=1)


def row_choice(row, start, count):
    index = lax.broadcasted_iota(jnp.int32, (count, row.shape[1]), 0) + start
    return jnp.where(index == row, 1.0, 0.0).astype(BF16)


def code_rows(recv, rows):
    return [
        jnp.concatenate([recv[h, k : k + 1, :rows] for h in range(recv.shape[0])], axis=1) for k in range(6)
    ]


def selections(position, codes, weight, innov):
    half = codes[0].shape[1]
    column = columns(position, 128)
    pick = lane_choice(column, 0, 2 * half)
    pick_t = jnp.concatenate([row_choice(position, i * half, half) for i in range(2)], axis=1)
    onehot, onehot_t = [], []
    for t in range(3):
        pair = codes[2 * t : 2 * t + 2]
        onehot.append(jnp.concatenate([lane_choice(columns(row, 128), 0, CODES) for row in pair], axis=1))
        onehot_t.append(jnp.concatenate([row_choice(row, 0, CODES) for row in pair], axis=1))
    high = weight.astype(BF16)
    tiles = jnp.concatenate([high, (weight - high.astype(F32)).astype(BF16)], axis=2)
    turned = innov.T
    return pick, pick_t, onehot, onehot_t, tiles, jnp.concatenate([turned, turned], axis=1)


def selections_kernel(rows, position, codes, weight, innov, pick, pick_t, onehot, onehot_t, tiles, turned):
    obs = position.shape[1]
    member = lax.axis_index("member")
    kept = weight[pl.ds(member * (obs // TILE), obs // TILE)]
    seen = innov[:, pl.ds(pl.multiple_of(member * obs, obs), obs)]
    made = selections(position[0:1], code_rows(codes, rows), kept, seen)
    pick[...], pick_t[...] = made[0], made[1]
    for t in range(3):
        onehot[t], onehot_t[t] = made[2][t], made[3][t]
    tiles[...], turned[...] = made[4], made[5]


def select_all(rows, position, codes, weight, innov):
    obs = position.shape[1]
    half = codes.shape[0] * rows
    if rows % 16:
        member = lax.axis_index("member")
        kept = lax.dynamic_slice_in_dim(weight, member * (obs // TILE), obs // TILE, 0)
        seen = lax.dynamic_slice_in_dim(innov, member * obs, obs, 1)
        pick, pick_t, onehot, onehot_t, tiles, turned = selections(
            position[0:1], code_rows(codes, rows), kept, seen
        )
        return pick, pick_t, jnp.stack(onehot), jnp.stack(onehot_t), tiles, turned
    lev = innov.shape[0]
    out = (
        shape((obs, 2 * half), BF16),
        shape((half, 2 * obs), BF16),
        shape((3, half, 2 * CODES), BF16),
        shape((3, CODES, 2 * half), BF16),
        shape((obs // TILE, TILE, 2 * TILE), BF16),
        shape((obs, 2 * lev), F32),
    )
    return call(functools.partial(selections_kernel, rows), out, [position, codes, weight, innov])


def turn_kernel(group, sign, *refs):
    near, far, adj_own, adj_other, base, pert, tables, vert, vert_t, vec, inc, inc_half, square = refs[:13]
    adj, acc, moved, mixed = refs[13:]
    rows = vert.shape[0]
    lev = rows // group
    adj[...] = adj_own[...] + adj_other[...].astype(F32)
    acc[...] = jnp.zeros_like(acc)
    square[...] = jnp.zeros_like(square)
    sources = (pert, near, far)

    def project(g):
        parts = []
        for t in range(3):
            values = sources[t][pl.ds(g * group, group)].astype(F32)
            parts.append(
                jnp.concatenate(
                    [(values[j, 0] * adj[t, 0] + values[j, 1] * adj[t, 1]).astype(BF16) for j in range(group)],
                    axis=0,
                )
            )
        moved[g] = dot(jnp.concatenate(parts, axis=1), tables[...], ((1,), (1,))).astype(BF16)

    def lift(g):
        at = pl.ds(g * group, group)
        new = base[at].reshape(rows, CELLS) + dot(vert_t[...], moved[g])
        if sign < 0:
            new = -new
        vec[at] = new.reshape(group, lev, CELLS)
        square[...] += jnp.sum((new * new).reshape(rows // 8, 8, CELLS), axis=0)

    def mix(g):
        half = vec[pl.ds(g * group, group)].reshape(rows, CELLS).astype(BF16)
        mixed[g] = dot(vert[...], half).astype(BF16)

    def gather(g):
        local = dot(mixed[g], tables[...])
        for t in range(3):
            values = sources[t][pl.ds(g * group, group)]
            for s in range(SLOTS):
                total = acc[t, s]
                for j in range(group):
                    part = local[j * lev : (j + 1) * lev, t * CELLS : (t + 1) * CELLS]
                    total += values[j, s].astype(F32) * part
                acc[t, s] = total

    stages = (gather, mix, lift, project)
    steps = base.shape[0] // group
    depth = len(stages)
    for i in range(min(depth - 1, steps)):
        for k, stage in enumerate(stages):
            if 0 <= i - (depth - 1 - k):
                stage(i - (depth - 1 - k))

    def step(g, _):
        for k, stage in enumerate(stages):
            stage(g - (depth - 1 - k))
        return 0

    lax.fori_loop(depth - 1, steps, step, 0)
    for i in range(max(steps, depth - 1), steps + depth - 1):
        for k, stage in enumerate(stages):
            if 0 <= i - (depth - 1 - k) < steps:
                stage(i - (depth - 1 - k))
    inc[...] = acc[...]
    inc_half[...] = acc[...].astype(BF16)


def turn(adj_own, adj_other, base, pert, near, far, tables, vert, vert_t, sign):
    count, lev, _ = base.shape
    group = vert.shape[0] // lev
    field = (3, SLOTS, lev, CELLS)
    out = (shape(base.shape, F32), shape(field, F32), shape(field, BF16), shape((8, CELLS), F32))
    half = pltpu.VMEM((count // group, group * lev, CELLS), BF16)
    return call(
        functools.partial(turn_kernel, group, sign),
        out,
        [near, far, adj_own, adj_other, base, pert, tables, vert, vert_t],
        [pltpu.VMEM(field, F32), pltpu.VMEM(field, F32), half, half],
    )


def three_pieces(row, rows):
    high = row.astype(BF16).astype(F32)
    mid = (row - high).astype(BF16).astype(F32)
    low = row - high - mid
    index = lax.broadcasted_iota(jnp.int32, (rows, row.shape[1]), 0)
    tile = jnp.where(index == 0, high, jnp.where(index == 1, mid, jnp.where(index == 2, low, 0.0)))
    return tile.astype(BF16)


def twice(cells):
    blank = jnp.zeros_like(cells)
    return jnp.concatenate(
        [jnp.concatenate([cells, blank], axis=1), jnp.concatenate([blank, cells], axis=1)], axis=0
    )


def scalar_row(values, width):
    lane = lax.broadcasted_iota(jnp.int32, (1, width), 1)
    row = jnp.zeros((1, width), F32)
    for i, value in enumerate(values):
        row = jnp.where(lane == i, value, row)
    return row


def sampled_rows(inc, other, onehot, t):
    total = (inc[t] + other[t].astype(F32)).astype(BF16)
    cells = jnp.concatenate([total[s] for s in range(SLOTS)], axis=1)
    return dot(onehot[t], twice(cells), ((1,), (1,))).astype(BF16)


def sample_kernel(regions, rows, kinds, inc, other, onehot, *refs):
    out = refs[-1]
    for t in range(kinds):
        found = sampled_rows(inc, other, onehot, t)
        for h in range(regions):
            out[h, t * rows : (t + 1) * rows] = found[h * rows : (h + 1) * rows]
    if len(refs) > 1:
        tile = three_pieces(scalar_row([jnp.sum(ref[...]) for ref in refs[:-1]], out.shape[2]), 8)
        for h in range(regions):
            out[h, kinds * rows :] = tile


def sample(regions, rows, inc, other, onehot, scal=()):
    kinds, lev = inc.shape[0], inc.shape[2]
    extra = 8 if scal else 0
    if rows % 16:
        parts = [sampled_rows(inc, other, onehot, t).reshape(regions, rows, 2 * lev) for t in range(kinds)]
        if scal:
            tile = three_pieces(scalar_row([jnp.sum(v) for v in scal], 2 * lev), 8)
            parts.append(jnp.broadcast_to(tile[None], (regions,) + tile.shape))
        return jnp.concatenate(parts, axis=1)
    return call(
        functools.partial(sample_kernel, regions, rows, kinds),
        shape((regions, kinds * rows + extra, 2 * lev), BF16),
        [inc, other, onehot, *scal],
    )


def gathered(regions, rows, kinds, recv):
    parts = []
    for e in range(regions):
        total = recv[e, 0:rows].astype(F32)
        for t in range(1, kinds):
            source = side(e, t, regions)
            if source is not None:
                total = total + recv[source, t * rows : (t + 1) * rows].astype(F32)
        parts.append(total)
    return jnp.concatenate(parts, axis=0)


def swap_lanes(values):
    half = values.shape[1] // 2
    return jnp.concatenate([values[:, half:], values[:, :half]], axis=1)


def departures(regions, rows, kinds, recv, pick):
    slots = gathered(regions, rows, kinds, recv)
    high = slots.astype(BF16).astype(F32)
    low = swap_lanes(slots - high)
    first = lax.broadcasted_iota(jnp.int32, slots.shape, 1) < slots.shape[1] // 2
    stacked = jnp.concatenate([jnp.where(first, high, low), jnp.where(first, low, high)], axis=0)
    found = dot(pick, stacked.astype(BF16))
    return found + swap_lanes(found)


def weigh(tiles, both):
    high = both.astype(BF16).astype(F32)
    first = lax.broadcasted_iota(jnp.int32, both.shape, 1) < both.shape[1] // 2
    split = jnp.where(first, high, both - high).astype(BF16)
    parts = []
    for i in range(tiles.shape[0]):
        own = split[i * TILE : (i + 1) * TILE]
        parts.append(dot(tiles[i], jnp.concatenate([own, own], axis=0)))
    out = jnp.concatenate(parts, axis=0)
    return out + swap_lanes(out)


def halves_apart(both):
    first = lax.broadcasted_iota(jnp.int32, both.shape, 1) < both.shape[1] // 2
    return jnp.concatenate([jnp.where(first, both, 0.0), jnp.where(first, 0.0, both)], axis=0).astype(BF16)


def column_sums(values):
    return jnp.sum(values.reshape(values.shape[0] // 8, 8, values.shape[1]), axis=0)


def weigh_kernel(regions, rows, kinds, recv, pick, pick_t, tiles, innov, out, dep_out, wgt_out, seen):
    dep = departures(regions, rows, kinds, recv, pick[...])
    if innov is not None:
        dep = dep - innov[...]
    wgt = weigh(tiles, dep)
    dep_out[...] = dep
    wgt_out[...] = wgt
    seen[...] = column_sums(0.5 * dep * wgt)
    back = dot(pick_t[...], halves_apart(wgt)).astype(BF16)
    for r in range(regions):
        for t in range(3):
            source = side(r, t, regions)
            if source is None:
                out[r, t * rows : (t + 1) * rows] = jnp.zeros((rows, back.shape[1]), BF16)
            else:
                out[r, t * rows : (t + 1) * rows] = back[source * rows : (source + 1) * rows]


def weigh_later_kernel(regions, rows, kinds, recv, pick, pick_t, tiles, out, dep_out, wgt_out, seen):
    weigh_kernel(regions, rows, kinds, recv, pick, pick_t, tiles, None, out, dep_out, wgt_out, seen)


def spread_regions(back, fill):
    regions = back.shape[0]
    tail = back.shape[1:]
    near = back.reshape((regions // 2, 2) + tail)[:, ::-1].reshape(back.shape)
    inner = back[1 : regions - 1].reshape((regions // 2 - 1, 2) + tail)[:, ::-1]
    blank = jnp.broadcast_to(fill, (1,) + tail)
    far = jnp.concatenate([blank, inner.reshape((regions - 2,) + tail), blank], axis=0)
    return jnp.concatenate([back, near, far], axis=1)


def weighed(regions, rows, recv, pick, pick_t, tiles, innov=None):
    lanes = recv.shape[2]
    kinds = recv.shape[1] // rows
    obs = pick.shape[0]
    if rows % 16:
        dep = departures(regions, rows, kinds, recv, pick)
        dep = dep if innov is None else dep - innov
        wgt = weigh(tiles, dep)
        back = dot(pick_t, halves_apart(wgt)).astype(BF16).reshape(regions, rows, lanes)
        return spread_regions(back, jnp.zeros((), BF16)), dep, wgt, column_sums(0.5 * dep * wgt)
    out = (
        shape((regions, 3 * rows, lanes), BF16),
        shape((obs, lanes), F32),
        shape((obs, lanes), F32),
        shape((8, lanes), F32),
    )
    args = [recv, pick, pick_t, tiles] + ([] if innov is None else [innov])
    kernel = weigh_later_kernel if innov is None else weigh_kernel
    return call(functools.partial(kernel, regions, rows, kinds), out, args)


def scattered_field(rows_t, onehot_t, lev):
    count = rows_t.shape[0]
    low = dot(onehot_t[:, :count], rows_t).T
    high = dot(onehot_t[:, count:], rows_t).T
    return low[:lev] + high[lev:]


def scatter_kernel(regions, rows, recv, onehot_t, out, half):
    lev = out.shape[2]
    for t in range(3):
        values = jnp.concatenate([recv[h, t * rows : (t + 1) * rows] for h in range(regions)], axis=0)
        field = scattered_field(values, onehot_t[t], lev)
        for s in range(SLOTS):
            piece = field[:, s * CELLS : (s + 1) * CELLS]
            out[t, s] = piece
            half[t, s] = piece.astype(BF16)


def scattered(regions, rows, recv, onehot_t):
    lanes = recv.shape[2]
    lev = lanes // 2
    if rows % 16:
        parts = []
        for t in range(3):
            values = recv[:, t * rows : (t + 1) * rows].reshape(regions * rows, lanes)
            field = scattered_field(values, onehot_t[t], lev)
            parts.append(jnp.stack([field[:, s * CELLS : (s + 1) * CELLS] for s in range(SLOTS)]))
        full = jnp.stack(parts)
        return full, full.astype(BF16)
    field = (3, SLOTS, lev, CELLS)
    return call(
        functools.partial(scatter_kernel, regions, rows),
        (shape(field, F32), shape(field, BF16)),
        [recv, onehot_t],
    )


def last_sums(regions, rows, recv, pick, tiles, dep, wgt, pieces, norms):
    total = jnp.sum(jnp.sum(pieces.astype(F32), axis=0), axis=0, keepdims=True)
    lane = lax.broadcasted_iota(jnp.int32, total.shape, 1)
    norm = jnp.sum(jnp.where(lane == 0, total, 0.0))
    seen = jnp.sum(jnp.where(lane == 1, total, 0.0))
    step = norm / (norm + seen)
    dep_image = departures(regions, rows, 3, recv, pick)
    dep_next = dep - step * dep_image
    wgt_next = weigh(tiles, dep_next)
    squares, mixed = norms(step)
    values = [
        squares,
        mixed,
        0.5 * jnp.sum(dep_next * wgt_next),
        0.5 * jnp.sum(dep_next * wgt),
    ]
    return scalar_row(values, 128), scalar_row([norm, seen, step], 128)


def last_kernel(regions, rows, group, recv, pick, tiles, dep, wgt, resid, image, out, known):
    count, lev, cells = resid.shape

    def norms(step):
        def add(g, carry):
            at = pl.ds(g * group, group)
            now = resid[at].reshape(group * lev, cells)
            later = now - step * image[at].reshape(group * lev, cells)
            return carry[0] + column_sums(later * later), carry[1] + column_sums(later * now)

        zero = jnp.zeros((8, cells), F32)
        squares, mixed = lax.fori_loop(0, count // group, add, (zero, zero))
        return jnp.sum(squares), jnp.sum(mixed)

    pieces = recv[:, 3 * rows : 3 * rows + 3]
    sums, facts = last_sums(regions, rows, recv, pick[...], tiles, dep[...], wgt[...], pieces, norms)
    wide = jnp.broadcast_to(sums, (8, 128))
    for r in range(regions):
        out[r] = wide
    known[...] = jnp.broadcast_to(facts, (8, 128))


def last(regions, rows, recv, pick, tiles, dep, wgt, resid, image):
    if rows % 16:

        def norms(step):
            later = resid - step * image
            return jnp.sum(later * later), jnp.sum(later * resid)

        sums, facts = last_sums(
            regions, rows, recv, pick, tiles, dep, wgt, recv[:, 3 * rows : 3 * rows + 3], norms
        )
        return jnp.broadcast_to(sums[None], (regions, 8, 128)), jnp.broadcast_to(facts, (8, 128))
    group = group_size(resid.shape[0])
    return call(
        functools.partial(last_kernel, regions, rows, group),
        (shape((regions, 8, 128), F32), shape((8, 128), F32)),
        [recv, pick, tiles, dep, wgt, resid, image],
    )


def finish(total, facts, emit):
    lane = lax.broadcasted_iota(jnp.int32, total.shape, 1)
    norm_next, mixed, seen_next, seen_mixed = (jnp.sum(jnp.where(lane == i, total, 0.0)) for i in range(4))
    norm, seen, step = (jnp.sum(jnp.where(lane == i, facts, 0.0)) for i in range(3))
    ratio = norm_next / norm
    curved = norm_next + seen_next + 2.0 * ratio * (mixed + seen_mixed) + ratio * ratio * (norm + seen)
    step_next = norm_next / curved
    along, across = step + step_next * (1.0 + ratio), step_next * step
    return emit(along, across)


def finish_kernel(group, sums, others, facts, control, resid, image, out):
    total = jnp.sum(sums[...] + others[...], axis=0)[0:1]

    def emit(along, across):
        def add(g, _):
            at = pl.ds(g * group, group)
            out[at] = control[at] + along * resid[at] - across * image[at]
            return 0

        lax.fori_loop(0, control.shape[0] // group, add, 0)

    finish(total, facts[0:1], emit)


def finished(sums, others, facts, control, resid, image):
    group = group_size(control.shape[0])
    return call(
        functools.partial(finish_kernel, group),
        jax.ShapeDtypeStruct(control.shape, F32),
        [sums, others, facts, control, resid, image],
    )


def to_regions(values):
    return lax.all_to_all(values, "region", split_axis=0, concat_axis=0, tiled=True)


def other_members(own, half):
    if lax.axis_size("member") == 2:
        return own, lax.ppermute(half, "member", [(0, 1), (1, 0)])
    return lax.psum(half, "member").astype(F32), jnp.zeros_like(half)


def member_sum(values):
    if lax.axis_size("member") == 2:
        return values + lax.ppermute(values, "member", [(0, 1), (1, 0)])
    return lax.psum(values, "member")


def local(
    perturbations,
    control,
    vertical_loc,
    block_kernels,
    loc_pattern,
    obs_region,
    obs_slot,
    obs_cell,
    innovations,
    obs_weight,
):
    regions = lax.axis_size("region")
    members = lax.axis_size("member")
    member = lax.axis_index("member")
    count, _, _ = control.shape
    obs = obs_region.shape[0] // members
    cap = max(2, 2 * obs // regions)

    chunks = HALO_CHUNKS if count % (4 * HALO_CHUNKS) == 0 else 1
    size = count // chunks
    group = group_size(size)

    near_p, far_p = halo([perturbations[i * size : (i + 1) * size] for i in range(chunks)])

    first = member * obs
    targets = lax.dynamic_slice_in_dim(obs_region[:, 0], first, obs, 0)
    codes = lax.dynamic_slice_in_dim(obs_slot * CELLS + obs_cell, first, obs, 0)
    named = targets[:, None] == jnp.arange(regions, dtype=jnp.int32)[None, :]
    lower = lax.broadcasted_iota(jnp.int32, (obs, obs), 0) > lax.broadcasted_iota(jnp.int32, (obs, obs), 1)
    earlier = dot(lower.astype(BF16), named.astype(BF16))
    rank = jnp.sum(jnp.where(named, earlier, 0.0), axis=1).astype(jnp.int32)
    rows = cap // 2
    slots_of_half = regions * rows
    position = (rank // rows) * slots_of_half + targets * rows + rank % rows
    slots = jnp.arange(2 * slots_of_half, dtype=jnp.int32)
    slot_codes = dot((slots[:, None] == position[None, :]).astype(BF16), (codes + 1).astype(BF16)[:, None])
    slot_codes = slot_codes[:, 0].astype(jnp.int32) - 1
    slot_codes = slot_codes.reshape(2, regions, rows).transpose(1, 0, 2)
    sent_codes = spread_regions(slot_codes, jnp.full((), -1, jnp.int32))
    sent_codes = jnp.pad(sent_codes, ((0, 0), (0, 2), (0, 128 - rows)))
    got_codes = to_regions(sent_codes)
    spots = jnp.broadcast_to(position[None], (8, obs))
    late = max(0, chunks - 2)
    got_codes, far_p[late] = lax.optimization_barrier((got_codes, far_p[late]))
    pick, pick_t, onehot, onehot_t, tiles, innov = select_all(
        rows, spots, got_codes, obs_weight, innovations
    )
    pick, far_p[-1] = lax.optimization_barrier((pick, far_p[-1]))

    own, lifted, tables, vert, vert_t = own_forward(
        loc_pattern, control, perturbations, block_kernels, vertical_loc, group
    )
    near, near_p = near_forward(near_p, lifted, tables, group)
    inc, half, far_p = far_forward(far_p, own, near, lifted, tables, group)
    inc, other = other_members(inc, half)
    recv = to_regions(sample(regions, rows, inc, other, onehot))
    back, _, _, _ = weighed(regions, rows, recv, pick, pick_t, tiles, innov)
    adj, adj_half = scattered(regions, rows, to_regions(back), onehot_t)
    adj, adj_other = other_members(adj, adj_half)
    resid, inc, half, square = turn(
        adj, adj_other, control, perturbations, near_p, far_p, tables, vert, vert_t, -1
    )

    inc, other = other_members(inc, half)
    recv = to_regions(sample(regions, rows, inc, other, onehot))
    back, dep, wgt, seen = weighed(regions, rows, recv, pick, pick_t, tiles)
    adj, adj_half = scattered(regions, rows, to_regions(back), onehot_t)
    adj, adj_other = other_members(adj, adj_half)
    square, seen = member_sum(square), member_sum(seen)
    image, inc, half, _ = turn(
        adj, adj_other, resid, perturbations, near_p, far_p, tables, vert, vert_t, 1
    )

    inc, other = other_members(inc, half)
    recv = to_regions(sample(regions, rows, inc, other, onehot, (square, seen)))
    sums, facts = last(regions, rows, recv, pick, tiles, dep, wgt, resid, image)
    sums, others = other_members(*[to_regions(sums)] * 2)
    return finished(sums, others, facts, control, resid, image)


def solution(mesh):
    placed = (
        P("member", None, None, "region"),
        P("member", None, "region"),
        P(),
        P(),
        P(),
        P("region", None),
        P("region"),
        P("region"),
        P(None, "region"),
        P("region", None, None),
    )

    return jax.shard_map(local, mesh=mesh, in_specs=placed, out_specs=P("member", None, "region"), check_vma=False)
```

profile of v0, /device:TPU:0, one launch (start us, length us, event | category | flops | bytes accessed | tf_op | source)
XLA Modules:
  0.0 184.5 jit_solution(2678632542362092518)
XLA Ops:
  0.0 2.3 %fusion.9 = (bf16[8,2,64,128]{3,2,1,0:T(8,128)(2,1)}, bf16[8,2,64,128]{3,2,1,0:T(8,128)(2,1)}, bf16[8,2,64,128]{3,2,1,0:T(8,128)(2,1)S(1)}, bf16[8,2,64,128]{3,2,1,0:T(8,128)(2,1)S(1)}, bf16[8,2,64,128]{3,2,1,0:T(8,128)(2,1)S(1)}) fusion(bf16[40,2,64,128]{3,2,1,0:T(8,128)(2,1)} %refs_5_.3), kind=kLoop, calls=%fused_computation.26 | loop fusion | bytes 2621440 | tf_op jit(solution)/shard_map/slice | solution.py:671
  2.3 3.0 %collective-permute-start.4 = (bf16[8,2,64,128]{3,2,1,0:T(8,128)(2,1)}, bf16[8,2,64,128]{3,2,1,0:T(8,128)(2,1)}, u32[]{:S(2)}, u32[]{:S(2)}) collective-permute-start(bf16[8,2,64,128]{3,2,1,0:T(8,128)(2,1)} %get-tuple-element.81), channel_id=1, source_target_pairs={{0,2},{2,0},{4,6},{6,4},{8,10},{10,8},{12,14},{14,12},{16,18},{18,... | collective-permute-start | bytes 786440 | tf_op jit(solution)/shard_map/ppermute | solution.py:42
  5.4 1.9 %collective-permute-start.2 = (bf16[8,2,64,128]{3,2,1,0:T(8,128)(2,1)S(1)}, bf16[8,2,64,128]{3,2,1,0:T(8,128)(2,1)}, u32[]{:S(2)}, u32[]{:S(2)}) collective-permute-start(bf16[8,2,64,128]{3,2,1,0:T(8,128)(2,1)S(1)} %get-tuple-element.83), channel_id=1, source_target_pairs={{0,2},{2,0},{4,6},{6,4},{8,10},{10,8},{12,14},{14,12},{16,18},{18,... | collective-permute-start | bytes 786440 | tf_op jit(solution)/shard_map/ppermute | solution.py:42
  7.5 1.9 %collective-permute-start = (bf16[8,2,64,128]{3,2,1,0:T(8,128)(2,1)S(1)}, bf16[8,2,64,128]{3,2,1,0:T(8,128)(2,1)}, u32[]{:S(2)}, u32[]{:S(2)}) collective-permute-start(bf16[8,2,64,128]{3,2,1,0:T(8,128)(2,1)S(1)} %get-tuple-element.85), channel_id=1, source_target_pairs={{0,2},{2,0},{4,6},{6,4},{8,10},{10,8},{12,14},{14,12},{16,18},{18,... | collective-permute-start | bytes 786440 | tf_op jit(solution)/shard_map/ppermute | solution.py:42
  10.3 2.5 %collective-permute-done.4.refs_4_ = bf16[8,2,64,128]{3,2,1,0:T(8,128)(2,1)} collective-permute-done((bf16[8,2,64,128]{3,2,1,0:T(8,128)(2,1)}, bf16[8,2,64,128]{3,2,1,0:T(8,128)(2,1)}, u32[]{:S(2)}, u32[]{:S(2)}) %collective-permute-start.4) | collective-permute-done | bytes 262176 | tf_op jit(solution)/shard_map/ppermute | solution.py:42
  12.8 4.7 %collective-permute-start.9 = (bf16[8,2,64,128]{3,2,1,0:T(8,128)(2,1)}, bf16[8,2,64,128]{3,2,1,0:T(8,128)(2,1)}, u32[]{:S(2)}, u32[]{:S(2)}) collective-permute-start(bf16[8,2,64,128]{3,2,1,0:T(8,128)(2,1)} %collective-permute-done.4.refs_4_), channel_id=1, source_target_pairs={{0,4},{4,8},{6,2},{8,12},{10,6},{12,16},{14,10},{16,20},{18,14},{2... | collective-permute-start | bytes 786440 | tf_op jit(solution)/shard_map/ppermute | solution.py:43
  18.5 4.7 %collective-permute-start.8 = (bf16[8,2,64,128]{3,2,1,0:T(8,128)(2,1)}, bf16[8,2,64,128]{3,2,1,0:T(8,128)(2,1)}, u32[]{:S(2)}, u32[]{:S(2)}) collective-permute-start(bf16[8,2,64,128]{3,2,1,0:T(8,128)(2,1)} %collective-permute-done.3.refs_3_), channel_id=1, source_target_pairs={{0,4},{4,8},{6,2},{8,12},{10,6},{12,16},{14,10},{16,20},{18,14},{2... | collective-permute-start | bytes 786440 | tf_op jit(solution)/shard_map/ppermute | solution.py:43
  24.1 4.7 %collective-permute-start.7 = (bf16[8,2,64,128]{3,2,1,0:T(8,128)(2,1)}, bf16[8,2,64,128]{3,2,1,0:T(8,128)(2,1)}, u32[]{:S(2)}, u32[]{:S(2)}) collective-permute-start(bf16[8,2,64,128]{3,2,1,0:T(8,128)(2,1)} %collective-permute-done.2.refs_2_), channel_id=1, source_target_pairs={{0,4},{4,8},{6,2},{8,12},{10,6},{12,16},{14,10},{16,20},{18,14},{2... | collective-permute-start | bytes 786440 | tf_op jit(solution)/shard_map/ppermute | solution.py:43
  29.7 4.7 %collective-permute-start.6 = (bf16[8,2,64,128]{3,2,1,0:T(8,128)(2,1)}, bf16[8,2,64,128]{3,2,1,0:T(8,128)(2,1)}, u32[]{:S(2)}, u32[]{:S(2)}) collective-permute-start(bf16[8,2,64,128]{3,2,1,0:T(8,128)(2,1)} %collective-permute-done.1.refs_1_), channel_id=1, source_target_pairs={{0,4},{4,8},{6,2},{8,12},{10,6},{12,16},{14,10},{16,20},{18,14},{2... | collective-permute-start | bytes 786440 | tf_op jit(solution)/shard_map/ppermute | solution.py:43
  34.5 4.4 %collective-permute-start.5 = (bf16[8,2,64,128]{3,2,1,0:T(8,128)(2,1)}, bf16[8,2,64,128]{3,2,1,0:T(8,128)(2,1)}, u32[]{:S(2)}, u32[]{:S(2)}) collective-permute-start(bf16[8,2,64,128]{3,2,1,0:T(8,128)(2,1)} %collective-permute-done.refs_0_), channel_id=1, source_target_pairs={{0,4},{4,8},{6,2},{8,12},{10,6},{12,16},{14,10},{16,20},{18,14},{2... | collective-permute-start | bytes 786440 | tf_op jit(solution)/shard_map/ppermute | solution.py:43
  39.6 5.9 %all-to-all-start = ((s32[16,8,128]{2,1,0:T(8,128)}), s32[16,8,128]{2,1,0:T(8,128)}, u32[]{:S(2)}, u32[]{:S(2)}) async-start(s32[16,8,128]{2,1,0:T(8,128)} %pad.4), calls=%async_computation | async-start | bytes 131072 | tf_op jit(solution)/shard_map/all_to_all | solution.py:633
  46.6 3.5 %shard_map.100 = (f32[2,64,128]{2,1,0:T(8,128)S(1)}, bf16[40,64,128]{2,1,0:T(8,128)(2,1)S(1)}, bf16[128,384]{1,0:T(8,128)(2,1)S(1)}, bf16[256,256]{1,0:T(8,128)(2,1)S(1)}, bf16[256,256]{1,0:T(8,128)(2,1)S(1)}) custom-call(s32[16,3]{1,0:T(8,128)S(1)} %copy.12.pattern, f32[40,64,128]{2,1,0:T(8,128)S(1)} %copy-done.2, bf16[40,2,64,128]{3,2,1,0:T(8,128)(2,1)S(1)} %copy-done.1, ...), custom_call_target="tpu_custom_call" | custom-call | tf_op jit(solution)/shard_map/pallas_call | solution.py:49
  51.4 1.8 shard_map.101
  56.9 2.7 %shard_map.102 = (bf16[512,1024]{1,0:T(8,128)(2,1)S(1)}, bf16[512,1024]{1,0:T(8,128)(2,1)S(1)}, bf16[3,512,512]{2,1,0:T(8,128)(2,1)S(1)}, bf16[3,256,1024]{2,1,0...) custom-call(s32[8,512]{1,0:T(8,128)S(1)} %broadcast_in_dim.10.position, ...), custom_call_target="tpu_custom_call" | custom-call | tf_op jit(solution)/shard_map/pallas_call | solution.py:49
  61.3 1.8 shard_map.103
  65.1 19.6 %all_to_all.35.recv = bf16[16,96,128]{2,1,0:T(8,128)(2,1)S(1)} all-to-all(bf16[16,96,128]{2,1,0:T(8,128)(2,1)S(1)} %shard_map.104), channel_id=1, replica_groups=mesh['region'=16,'member'=2] {'region'}, dimensions={0} | all-to-all | bytes 786432 | tf_op jit(solution)/shard_map/all_to_all | solution.py:633
  84.6 1.8 shard_map.105
  86.4 15.6 %all_to_all.36.recv = bf16[16,96,128]{2,1,0:T(8,128)(2,1)S(1)} all-to-all(bf16[16,96,128]{2,1,0:T(8,128)(2,1)S(1)} %get-tuple-element.60), channel_id=1, replica_groups=mesh['region'=16,'member'=2] {'region'}, dimensions={0} | all-to-all | bytes 786432 | tf_op jit(solution)/shard_map/all_to_all | solution.py:633
  104.0 4.2 %shard_map.107 = (f32[40,64,128]{2,1,0:T(8,128)S(1)}, f32[3,2,64,128]{3,2,1,0:T(8,128)S(1)}, bf16[3,2,64,128]{3,2,1,0:T(8,128)(2,1)S(1)}, f32[8,128]{1,0:T(8,128)S(1)}) custom-call(bf16[40,2,64,128]{3,2,1,0:T(8,128)(2,1)S(1)} %copy-done.4, bf16[40,2,64,128]{3,2,1,0:T(8,128)(2,1)S(1)} %get-tuple-element.52.refs_1_, ...), custom_call_target="tpu_custom_call" | custom-call | tf_op jit(solution)/shard_map/pallas_call | solution.py:49
  110.2 16.3 %all_to_all.37.recv = bf16[16,96,128]{2,1,0:T(8,128)(2,1)S(1)} all-to-all(bf16[16,96,128]{2,1,0:T(8,128)(2,1)S(1)} %shard_map.108), channel_id=1, replica_groups=mesh['region'=16,'member'=2] {'region'}, dimensions={0} | all-to-all | bytes 786432 | tf_op jit(solution)/shard_map/all_to_all | solution.py:633
  128.1 15.5 %all_to_all.38.recv = bf16[16,96,128]{2,1,0:T(8,128)(2,1)S(1)} all-to-all(bf16[16,96,128]{2,1,0:T(8,128)(2,1)S(1)} %get-tuple-element.68), channel_id=1, replica_groups=mesh['region'=16,'member'=2] {'region'}, dimensions={0} | all-to-all | bytes 786432 | tf_op jit(solution)/shard_map/all_to_all | solution.py:633
  145.6 4.4 %shard_map.111 = (f32[40,64,128]{2,1,0:T(8,128)S(1)}, f32[3,2,64,128]{3,2,1,0:T(8,128)S(1)}, bf16[3,2,64,128]{3,2,1,0:T(8,128)(2,1)S(1)}, f32[8,128]{1,0:T(8,128)}) custom-call(bf16[40,2,64,128]{3,2,1,0:T(8,128)(2,1)S(1)} %copy-done.4, bf16[40,2,64,128]{3,2,1,0:T(8,128)(2,1)S(1)} %get-tuple-element.52.refs_1_, ...), custom_call_target="tpu_custom_call" | custom-call | tf_op jit(solution)/shard_map/pallas_call | solution.py:49
  152.2 17.0 %all_to_all.39.recv = bf16[16,104,128]{2,1,0:T(8,128)(2,1)S(1)} all-to-all(bf16[16,104,128]{2,1,0:T(8,128)(2,1)S(1)} %shard_map.112), channel_id=1, replica_groups=mesh['region'=16,'member'=2] {'region'}, dimensions={0} | all-to-all | bytes 851968 | tf_op jit(solution)/shard_map/all_to_all | solution.py:633
  170.7 11.0 %all_to_all.40.sums = f32[16,8,128]{2,1,0:T(8,128)S(1)} all-to-all(f32[16,8,128]{2,1,0:T(8,128)S(1)} %get-tuple-element.79), channel_id=1, replica_groups=mesh['region'=16,'member'=2] {'region'}, dimensions={0} | all-to-all | bytes 131072 | tf_op jit(solution)/shard_map/all_to_all | solution.py:633
  (92 shorter events, 28.3 us)
Async XLA Ops:
  0.0 45.6 %copy-start.2 = (f32[40,64,128]{2,1,0:T(8,128)S(1)}, f32[40,64,128]{2,1,0:T(8,128)}, u32[]{:S(2)}) copy-start(f32[40,64,128]{2,1,0:T(8,128)} %control.1) | copy-start | bytes 3932164
  2.3 43.2 %copy-start.17 = (s32[16,3]{0,1:T(4,128)S(1)}, s32[16,3]{0,1:T(4,128)}, u32[]{:S(2)}) copy-start(s32[16,3]{0,1:T(4,128)} %param.14) | copy-start | bytes 580
  2.3 43.3 %copy-start.1 = (bf16[40,2,64,128]{3,2,1,0:T(8,128)(2,1)S(1)}, bf16[40,2,64,128]{3,2,1,0:T(8,128)(2,1)}, u32[]{:S(2)}) copy-start(bf16[40,2,64,128]{3,2,1,0:T(8,128)(2,1)} %refs_5_.3) | copy-start | bytes 3932164
  2.3 43.3 %copy-start.14 = (bf16[64,64]{1,0:T(8,128)(2,1)S(1)}, bf16[64,64]{1,0:T(8,128)(2,1)}, u32[]{:S(2)}) copy-start(bf16[64,64]{1,0:T(8,128)(2,1)} %vloc.1) | copy-start | bytes 24580
  2.3 10.5 %collective-permute-start.4 = (bf16[8,2,64,128]{3,2,1,0:T(8,128)(2,1)}, bf16[8,2,64,128]{3,2,1,0:T(8,128)(2,1)}, u32[]{:S(2)}, u32[]{:S(2)}) collective-permute-start(bf16[8,2,64,128]{3,2,1,0:T(8,128)(2,1)} %get-tuple-element.81), channel_id=1, source_target_pairs={{0,2},{2,0},{4,6},{6,4},{8,10},{10,8},{12,14},{14,12},{16,18},{18,... | collective-permute-start | bytes 786440 | tf_op jit(solution)/shard_map/ppermute | solution.py:42
  5.4 13.1 %collective-permute-start.3 = (bf16[8,2,64,128]{3,2,1,0:T(8,128)(2,1)}, bf16[8,2,64,128]{3,2,1,0:T(8,128)(2,1)}, u32[]{:S(2)}, u32[]{:S(2)}) collective-permute-start(bf16[8,2,64,128]{3,2,1,0:T(8,128)(2,1)} %get-tuple-element.82), channel_id=1, source_target_pairs={{0,2},{2,0},{4,6},{6,4},{8,10},{10,8},{12,14},{14,12},{16,18},{18,... | collective-permute-start | bytes 786440 | tf_op jit(solution)/shard_map/ppermute | solution.py:42
  5.4 18.6 %collective-permute-start.2 = (bf16[8,2,64,128]{3,2,1,0:T(8,128)(2,1)S(1)}, bf16[8,2,64,128]{3,2,1,0:T(8,128)(2,1)}, u32[]{:S(2)}, u32[]{:S(2)}) collective-permute-start(bf16[8,2,64,128]{3,2,1,0:T(8,128)(2,1)S(1)} %get-tuple-element.83), channel_id=1, source_target_pairs={{0,2},{2,0},{4,6},{6,4},{8,10},{10,8},{12,14},{14,12},{16,18},{18,... | collective-permute-start | bytes 786440 | tf_op jit(solution)/shard_map/ppermute | solution.py:42
  7.4 22.3 %collective-permute-start.1 = (bf16[8,2,64,128]{3,2,1,0:T(8,128)(2,1)S(1)}, bf16[8,2,64,128]{3,2,1,0:T(8,128)(2,1)}, u32[]{:S(2)}, u32[]{:S(2)}) collective-permute-start(bf16[8,2,64,128]{3,2,1,0:T(8,128)(2,1)S(1)} %get-tuple-element.84), channel_id=1, source_target_pairs={{0,2},{2,0},{4,6},{6,4},{8,10},{10,8},{12,14},{14,12},{16,18},{18,... | collective-permute-start | bytes 786440 | tf_op jit(solution)/shard_map/ppermute | solution.py:42
  7.5 27.0 %collective-permute-start = (bf16[8,2,64,128]{3,2,1,0:T(8,128)(2,1)S(1)}, bf16[8,2,64,128]{3,2,1,0:T(8,128)(2,1)}, u32[]{:S(2)}, u32[]{:S(2)}) collective-permute-start(bf16[8,2,64,128]{3,2,1,0:T(8,128)(2,1)S(1)} %get-tuple-element.85), channel_id=1, source_target_pairs={{0,2},{2,0},{4,6},{6,4},{8,10},{10,8},{12,14},{14,12},{16,18},{18,... | collective-permute-start | bytes 786440 | tf_op jit(solution)/shard_map/ppermute | solution.py:42
  12.8 46.7 %collective-permute-start.9 = (bf16[8,2,64,128]{3,2,1,0:T(8,128)(2,1)}, bf16[8,2,64,128]{3,2,1,0:T(8,128)(2,1)}, u32[]{:S(2)}, u32[]{:S(2)}) collective-permute-start(bf16[8,2,64,128]{3,2,1,0:T(8,128)(2,1)} %collective-permute-done.4.refs_4_), channel_id=1, source_target_pairs={{0,4},{4,8},{6,2},{8,12},{10,6},{12,16},{14,10},{16,20},{18,14},{2... | collective-permute-start | bytes 786440 | tf_op jit(solution)/shard_map/ppermute | solution.py:43
  18.5 36.4 %collective-permute-start.8 = (bf16[8,2,64,128]{3,2,1,0:T(8,128)(2,1)}, bf16[8,2,64,128]{3,2,1,0:T(8,128)(2,1)}, u32[]{:S(2)}, u32[]{:S(2)}) collective-permute-start(bf16[8,2,64,128]{3,2,1,0:T(8,128)(2,1)} %collective-permute-done.3.refs_3_), channel_id=1, source_target_pairs={{0,4},{4,8},{6,2},{8,12},{10,6},{12,16},{14,10},{16,20},{18,14},{2... | collective-permute-start | bytes 786440 | tf_op jit(solution)/shard_map/ppermute | solution.py:43
  24.1 35.5 %collective-permute-start.7 = (bf16[8,2,64,128]{3,2,1,0:T(8,128)(2,1)}, bf16[8,2,64,128]{3,2,1,0:T(8,128)(2,1)}, u32[]{:S(2)}, u32[]{:S(2)}) collective-permute-start(bf16[8,2,64,128]{3,2,1,0:T(8,128)(2,1)} %collective-permute-done.2.refs_2_), channel_id=1, source_target_pairs={{0,4},{4,8},{6,2},{8,12},{10,6},{12,16},{14,10},{16,20},{18,14},{2... | collective-permute-start | bytes 786440 | tf_op jit(solution)/shard_map/ppermute | solution.py:43
  29.7 29.9 %collective-permute-start.6 = (bf16[8,2,64,128]{3,2,1,0:T(8,128)(2,1)}, bf16[8,2,64,128]{3,2,1,0:T(8,128)(2,1)}, u32[]{:S(2)}, u32[]{:S(2)}) collective-permute-start(bf16[8,2,64,128]{3,2,1,0:T(8,128)(2,1)} %collective-permute-done.1.refs_1_), channel_id=1, source_target_pairs={{0,4},{4,8},{6,2},{8,12},{10,6},{12,16},{14,10},{16,20},{18,14},{2... | collective-permute-start | bytes 786440 | tf_op jit(solution)/shard_map/ppermute | solution.py:43
  34.5 25.1 %collective-permute-start.5 = (bf16[8,2,64,128]{3,2,1,0:T(8,128)(2,1)}, bf16[8,2,64,128]{3,2,1,0:T(8,128)(2,1)}, u32[]{:S(2)}, u32[]{:S(2)}) collective-permute-start(bf16[8,2,64,128]{3,2,1,0:T(8,128)(2,1)} %collective-permute-done.refs_0_), channel_id=1, source_target_pairs={{0,4},{4,8},{6,2},{8,12},{10,6},{12,16},{14,10},{16,20},{18,14},{2... | collective-permute-start | bytes 786440 | tf_op jit(solution)/shard_map/ppermute | solution.py:43
  39.6 15.2 %all-to-all-start = ((s32[16,8,128]{2,1,0:T(8,128)}), s32[16,8,128]{2,1,0:T(8,128)}, u32[]{:S(2)}, u32[]{:S(2)}) async-start(s32[16,8,128]{2,1,0:T(8,128)} %pad.4), calls=%async_computation | async-start | bytes 131072 | tf_op jit(solution)/shard_map/all_to_all | solution.py:633
  63.1 1.4 collective-permute-start.10
  86.4 17.6 %copy-start.6 = (bf16[256,256]{1,0:T(8,128)(2,1)S(1)}, bf16[256,256]{1,0:T(8,128)(2,1)}, u32[]{:S(2)}) copy-start(bf16[256,256]{1,0:T(8,128)(2,1)} %copy-done.5) | copy-start | bytes 393220
  102.6 1.4 collective-permute-start.11
  108.2 1.4 collective-permute-start.12
  144.2 1.4 collective-permute-start.13
  149.9 1.7 collective-permute-start.14
  150.1 1.2 collective-permute-start.15
  150.4 1.2 collective-permute-start.16
  181.8 1.3 collective-permute-start.17
  (13 other events, 54.0 us)
where the time goes:
time: 185 us
  blocking collectives  95 us (51%)
  starting transfers between devices  37.1 us (20%)
  Pallas kernels  27.8 us (15%)
  waiting for transfers between devices  12.8 us (7%)
  local copies, waits for them, and re-layouts  10.6 us (6%)
    all_to_all x6, blocking collectives, to_regions(): lax.all_to_all(values, 'region', split_axis=0, concat_axis=0, tiled=True)  95 us
    pallas_call x15, Pallas kernels, call(): pl.pallas_call(kernel, out_shape=out_shape, in_specs=[pl.BlockSpec(memory...  27.8 us
    ppermute x5, starting transfers between devices, halo(): far = [lax.ppermute(c, 'region', onward) for c in near]  23 us
    unnamed x37, local copies, waits for them, and re-layouts  7.6 us
    ppermute x5, starting transfers between devices, halo(): near = [lax.ppermute(c, 'region', pairs) for c in chunks]  7.09 us
    ppermute x6, waiting for transfers between devices, other_members(): return (own, lax.ppermute(half, 'member', [(0, 1), (1, 0)]))  6.27 us
    all_to_all x1, starting transfers between devices, to_regions(): lax.all_to_all(values, 'region', split_axis=0, concat_axis=0, tiled=True)  5.9 us
    ppermute x5, waiting for transfers between devices, halo(): near = [lax.ppermute(c, 'region', pairs) for c in chunks]  5.52 us
  transfers between devices with their start and end apart: 19, of which 12 were waited for; matrix products, arithmetic and copies ran while one was open for 1% of the time, Pallas kernels for 4%

commit v1 on v0

--- a/solution.py
+++ b/solution.py
@@ -14,7 +14,7 @@
 CODES = SLOTS * CELLS
 F32 = jnp.float32
 BF16 = jnp.bfloat16
-HALO_CHUNKS = 5
+HALO_SHARES = (2, 3, 3, 2)
 
 
 def near_of(r):
@@ -39,12 +39,15 @@
     pairs = [(r, r ^ 1) for r in range(regions)]
     onward = [(r, r + 2 if r % 2 == 0 else r - 2) for r in range(regions)]
     onward = [(s, d) for s, d in onward if 0 <= d < regions]
-    near = [lax.ppermute(c, "region", pairs) for c in chunks]
-    far = [lax.ppermute(c, "region", onward) for c in near]
+    near, far = [], []
+    for chunk in chunks:
+        near.append(lax.ppermute(chunk, "region", pairs))
+    for chunk in near:
+        far.append(lax.ppermute(chunk, "region", onward))
     return near, far
 
 
-def call(kernel, out_shape, args, scratch=(), limit=16, scalars=()):
+def call(kernel, out_shape, args, scratch=(), limit=16, scalars=(), aliases=None):
     vmem = pl.BlockSpec(memory_space=pltpu.VMEM)
     return pl.pallas_call(
         kernel,
@@ -52,8 +55,17 @@
         in_specs=[pl.BlockSpec(memory_space=pltpu.SMEM)] * len(scalars) + [vmem] * len(args),
         out_specs=jax.tree.map(lambda _: vmem, out_shape),
         scratch_shapes=list(scratch),
+        input_output_aliases=aliases or {},
         compiler_params=pltpu.CompilerParams(vmem_limit_bytes=limit << 20),
     )(*scalars, *[pltpu.with_memory_space_constraint(a, pltpu.VMEM) for a in args])
+
+
+def halo_sizes(groups):
+    whole = sum(HALO_SHARES)
+    ends = sorted({max(1, groups * sum(HALO_SHARES[: i + 1]) // whole) for i in range(len(HALO_SHARES))})
+    if len(ends) < 2:
+        ends = [1, groups]
+    return [b - a for a, b in zip([0] + ends, ends)]
 
 
 def group_size(members):
@@ -92,19 +104,30 @@
     for t in range(3):
         tables[:, t * CELLS : (t + 1) * CELLS] = kernels[picks[t]]
 
-    def step(g, _):
+    def mix(g):
         at = pl.ds(g * group, group)
         mixed = dot(vert[...], start[at].reshape(rows, CELLS).astype(BF16)).astype(BF16)
         lifted[at] = mixed.reshape(group, lev, CELLS)
-        local = dot(mixed, tables[:, :CELLS])
+
+    def gather(g):
+        at = pl.ds(g * group, group)
+        local = dot(lifted[at].reshape(rows, CELLS), tables[:, :CELLS])
+        values = pert[at]
         for s in range(SLOTS):
             total = acc[s]
             for j in range(group):
-                total += pert[g * group + j, s].astype(F32) * local[j * lev : (j + 1) * lev]
+                total += values[j, s].astype(F32) * local[j * lev : (j + 1) * lev]
             acc[s] = total
+
+    def step(g, _):
+        gather(g - 1)
+        mix(g)
         return 0
 
-    lax.fori_loop(0, count // group, step, 0, unroll=2)
+    steps = count // group
+    mix(0)
+    lax.fori_loop(1, steps, step, 0, unroll=3 if steps % 3 == 1 else 1)
+    gather(steps - 1)
     inc[...] = acc[...]
 
 
@@ -122,18 +145,16 @@
     )
 
 
-def part_sum(n, group, t, chunks, lifted, tables, acc, full):
+def part_sum(first, group, t, chunks, lifted, tables, acc, full):
     lev = lifted.shape[1]
     rows = group * lev
-    acc[...] = jnp.zeros_like(acc)
-    first = 0
-    for ch in range(n):
-        size = chunks[ch].shape[0]
-
-        def step(g, _, ch=ch, first=first):
+    for chunk in chunks:
+        size = chunk.shape[0]
+
+        def step(g, _, chunk=chunk, first=first):
             at = pl.ds(first + g * group, group)
             local = dot(lifted[at].reshape(rows, CELLS), tables[:, t * CELLS : (t + 1) * CELLS])
-            values = chunks[ch][pl.ds(g * group, group)]
+            values = chunk[pl.ds(g * group, group)]
             full[at] = values
             for s in range(SLOTS):
                 total = acc[s]
@@ -146,44 +167,36 @@
         first += size
 
 
-def near_kernel(n, group, *refs):
+def begin_kernel(n, group, t, *refs):
     chunks = refs[:n]
-    lifted, tables, inc, full, acc = refs[n:]
-    part_sum(n, group, 1, chunks, lifted, tables, acc, full)
-    inc[...] = acc[...]
-
-
-def joined(chunks):
-    return shape((sum(c.shape[0] for c in chunks),) + chunks[0].shape[1:], chunks[0].dtype)
-
-
-def near_forward(chunks, lifted, tables, group):
-    field = (SLOTS, lifted.shape[1], CELLS)
-    return call(
-        functools.partial(near_kernel, len(chunks), group),
-        (shape(field, F32), joined(chunks)),
-        [*chunks, lifted, tables],
-        [pltpu.VMEM(field, F32)],
-    )
-
-
-def far_kernel(n, group, *refs):
-    chunks = refs[:n]
-    own, near, lifted, tables, inc, half, full, acc = refs[n:]
-    part_sum(n, group, 2, chunks, lifted, tables, acc, full)
+    lifted, tables, inc, full = refs[n:]
+    inc[...] = jnp.zeros_like(inc)
+    part_sum(0, group, t, chunks, lifted, tables, inc, full)
+
+
+def begin_part(chunks, t, lifted, tables, group):
+    count, lev, cells = lifted.shape
+    out = (shape((SLOTS, lev, cells), F32), shape((count,) + chunks[0].shape[1:], chunks[0].dtype))
+    return call(functools.partial(begin_kernel, len(chunks), group, t), out, [*chunks, lifted, tables])
+
+
+def end_kernel(first, group, full_in, chunk, own, near, begun, lifted, tables, full, inc, half, acc):
+    del full_in
+    acc[...] = begun[...]
+    if chunk is not None:
+        part_sum(first, group, 2, [chunk], lifted, tables, acc, full)
     for t, part in enumerate((own, near, acc)):
         inc[t] = part[...]
         half[t] = part[...].astype(BF16)
 
 
-def far_forward(chunks, own, near, lifted, tables, group):
-    field = (SLOTS, lifted.shape[1], CELLS)
-    return call(
-        functools.partial(far_kernel, len(chunks), group),
-        (shape((3,) + field, F32), shape((3,) + field, BF16), joined(chunks)),
-        [*chunks, own, near, lifted, tables],
-        [pltpu.VMEM(field, F32)],
-    )
+def end_parts(chunk, own, near, begun, full, lifted, tables, group):
+    count, lev, cells = lifted.shape
+    field = (SLOTS, lev, cells)
+    out = (shape(full.shape, full.dtype), shape((3,) + field, F32), shape((3,) + field, BF16))
+    args = [full, chunk, own, near, begun, lifted, tables]
+    kernel = functools.partial(end_kernel, count - chunk.shape[0], group)
+    return call(kernel, out, args, [pltpu.VMEM(field, F32)], aliases={0: 0})
 
 
 def columns(row, width):
@@ -664,11 +677,12 @@
     obs = obs_region.shape[0] // members
     cap = max(2, 2 * obs // regions)
 
-    chunks = HALO_CHUNKS if count % (4 * HALO_CHUNKS) == 0 else 1
-    size = count // chunks
-    group = group_size(size)
-
-    near_p, far_p = halo([perturbations[i * size : (i + 1) * size] for i in range(chunks)])
+    group = group_size(count)
+    sizes = halo_sizes(count // group)
+    starts = [sum(sizes[:i]) * group for i in range(len(sizes) + 1)]
+    rest = lax.optimization_barrier(perturbations)
+    pieces = [(rest if i else perturbations)[starts[i] : starts[i + 1]] for i in range(len(sizes))]
+    near_p, far_p = halo(pieces)
 
     first = member * obs
     targets = lax.dynamic_slice_in_dim(obs_region[:, 0], first, obs, 0)
@@ -688,8 +702,7 @@
     sent_codes = jnp.pad(sent_codes, ((0, 0), (0, 2), (0, 128 - rows)))
     got_codes = to_regions(sent_codes)
     spots = jnp.broadcast_to(position[None], (8, obs))
-    late = max(0, chunks - 2)
-    got_codes, far_p[late] = lax.optimization_barrier((got_codes, far_p[late]))
+    got_codes, loc_pattern = lax.optimization_barrier((got_codes, loc_pattern))
     pick, pick_t, onehot, onehot_t, tiles, innov = select_all(
         rows, spots, got_codes, obs_weight, innovations
     )
@@ -698,8 +711,9 @@
     own, lifted, tables, vert, vert_t = own_forward(
         loc_pattern, control, perturbations, block_kernels, vertical_loc, group
     )
-    near, near_p = near_forward(near_p, lifted, tables, group)
-    inc, half, far_p = far_forward(far_p, own, near, lifted, tables, group)
+    near, near_p = begin_part(near_p, 1, lifted, tables, group)
+    begun, joined = begin_part(far_p[:-1], 2, lifted, tables, group)
+    far_p, inc, half = end_parts(far_p[-1], own, near, begun, joined, lifted, tables, group)
     inc, other = other_members(inc, half)
     recv = to_regions(sample(regions, rows, inc, other, onehot))
     back, _, _, _ = weighed(regions, rows, recv, pick, pick_t, tiles, innov)

time: 185 us -> 179 us (0.968)
  starting transfers between devices: 37.1 us -> 23.2 us
  blocking collectives: 95 us -> 104 us
  local copies, waits for them, and re-layouts: 10.6 us -> 5.83 us
  waiting for transfers between devices: 12.8 us -> 17 us
    all_to_all x6 -> x7, blocking collectives: 95 us -> 104 us  [to_regions(): lax.all_to_all(values, 'region', split_axis=0, concat_axis=0, tiled=True)]
    ppermute x10 -> x8, starting transfers between devices: 30.1 us -> 22.1 us  [the longest x4 17 us: halo(): far.append(lax.ppermute(chunk, 'region', onward))]
    unnamed x37 -> x20, local copies, waits for them, and re-layouts: 7.6 us -> 0.93 us
    all_to_all x1 -> x0, starting transfers between devices: 5.9 us -> none  [to_regions(): lax.all_to_all(values, 'region', split_axis=0, concat_axis=0, tiled=True)]
    ppermute x10 -> x8, waiting for transfers between devices: 5.53 us -> 9.72 us  [the longest x4 9.71 us: halo(): near.append(lax.ppermute(chunk, 'region', pairs))]
    slice x1 -> x3, local copies, waits for them, and re-layouts: 2.31 us -> 4.69 us  [local(): (rest if i else perturbations)[starts[i]:starts[i + 1]]]
    pallas_call x15 -> x16, Pallas kernels: 27.8 us -> 27.2 us  [call(): pl.pallas_call(kernel, out_shape=out_shape, in_specs=[pl.BlockSpec(memory...]
  transfers between devices with their start and end apart: 19 -> 16, of which waited for: 12 -> 11; matrix products, arithmetic and copies ran while one was open for 1% -> 2% of each run, Pallas kernels for 4% -> 4%
where the time goes in v1:
time: 179 us
  blocking collectives  104 us (58%)
  Pallas kernels  27.2 us (15%)
  starting transfers between devices  23.2 us (13%)
  waiting for transfers between devices  17 us (9%)
  local copies, waits for them, and re-layouts  5.83 us (3%)
    all_to_all x7, blocking collectives, to_regions(): lax.all_to_all(values, 'region', split_axis=0, concat_axis=0, tiled=True)  104 us
    pallas_call x16, Pallas kernels, call(): pl.pallas_call(kernel, out_shape=out_shape, in_specs=[pl.BlockSpec(memory...  27.2 us
    ppermute x4, starting transfers between devices, halo(): far.append(lax.ppermute(chunk, 'region', onward))  17 us
    ppermute x4, waiting for transfers between devices, halo(): near.append(lax.ppermute(chunk, 'region', pairs))  9.71 us
    ppermute x6, waiting for transfers between devices, other_members(): return (own, lax.ppermute(half, 'member', [(0, 1), (1, 0)]))  6.27 us
    ppermute x4, starting transfers between devices, halo(): near.append(lax.ppermute(chunk, 'region', pairs))  5.15 us
    slice x3, local copies, waits for them, and re-layouts, local(): (rest if i else perturbations)[starts[i]:starts[i + 1]]  4.69 us
  transfers between devices with their start and end apart: 16, of which 11 were waited for; matrix products, arithmetic and copies ran while one was open for 2% of the time, Pallas kernels for 4%

profile of v1, /device:TPU:0, one launch (start us, length us, event | category | flops | bytes accessed | tf_op | source)
XLA Modules:
  0.0 178.9 jit_solution(18246425648966093948)
XLA Ops:
  0.0 1.7 slice.15
  1.7 3.0 %collective-permute-start = (bf16[8,2,64,128]{3,2,1,0:T(8,128)(2,1)}, bf16[8,2,64,128]{3,2,1,0:T(8,128)(2,1)}, u32[]{:S(2)}, u32[]{:S(2)}) collective-permute-start(bf16[8,2,64,128]{3,2,1,0:T(8,128)(2,1)} %slice.15), channel_id=1, source_target_pairs={{0,2},{2,0},{4,6},{6,4},{8,10},{10,8},{12,14},{14,12},{16,18},{18,... | collective-permute-start | bytes 786440 | tf_op jit(solution)/shard_map/ppermute | solution.py:44
  4.7 1.7 slice.22
  7.8 1.9 %collective-permute-start.2 = (bf16[12,2,64,128]{3,2,1,0:T(8,128)(2,1)S(1)}, bf16[12,2,64,128]{3,2,1,0:T(8,128)(2,1)}, u32[]{:S(2)}, u32[]{:S(2)}) collective-permute-start(bf16[12,2,64,128]{3,2,1,0:T(8,128)(2,1)S(1)} %get-tuple-element.85), channel_id=1, source_target_pairs={{0,2},{2,0},{4,6},{6,4},{8,10},{10,8},{12,14},{14,12},{16,18},{18,... | collective-permute-start | bytes 1179656 | tf_op jit(solution)/shard_map/ppermute | solution.py:44
  12.1 4.7 %collective-permute-start.4 = (bf16[8,2,64,128]{3,2,1,0:T(8,128)(2,1)}, bf16[8,2,64,128]{3,2,1,0:T(8,128)(2,1)}, u32[]{:S(2)}, u32[]{:S(2)}) collective-permute-start(bf16[8,2,64,128]{3,2,1,0:T(8,128)(2,1)} %collective-permute-done.refs_0_), channel_id=1, source_target_pairs={{0,4},{4,8},{6,2},{8,12},{10,6},{12,16},{14,10},{16,20},{18,14},{2... | collective-permute-start | bytes 786440 | tf_op jit(solution)/shard_map/ppermute | solution.py:46
  17.7 4.7 %collective-permute-start.7 = (bf16[8,2,64,128]{3,2,1,0:T(8,128)(2,1)}, bf16[8,2,64,128]{3,2,1,0:T(8,128)(2,1)}, u32[]{:S(2)}, u32[]{:S(2)}) collective-permute-start(bf16[8,2,64,128]{3,2,1,0:T(8,128)(2,1)} %collective-permute-done.3.refs_3_), channel_id=1, source_target_pairs={{0,4},{4,8},{6,2},{8,12},{10,6},{12,16},{14,10},{16,20},{18,14},{2... | collective-permute-start | bytes 786440 | tf_op jit(solution)/shard_map/ppermute | solution.py:46
  22.4 3.8 %collective-permute-done.2.refs_2_ = bf16[12,2,64,128]{3,2,1,0:T(8,128)(2,1)} collective-permute-done((bf16[12,2,64,128]{3,2,1,0:T(8,128)(2,1)S(1)}, bf16[12,2,64,128]{3,2,1,0:T(8,128)(2,1)}, u32[]{:S(2)}, u32[]{:S(2)}) %collective-permute-start.2) | collective-permute-done | bytes 393248 | tf_op jit(solution)/shard_map/ppermute | solution.py:44
  26.2 4.0 %collective-permute-start.6 = (bf16[12,2,64,128]{3,2,1,0:T(8,128)(2,1)}, bf16[12,2,64,128]{3,2,1,0:T(8,128)(2,1)S(1)}, u32[]{:S(2)}, u32[]{:S(2)}) collective-permute-start(bf16[12,2,64,128]{3,2,1,0:T(8,128)(2,1)} %collective-permute-done.2.refs_2_), channel_id=1, source_target_pairs={{0,4},{4,8},{6,2},{8,12},{10,6},{12,16},{14,10},{16,20},{18,14},{2... | collective-permute-start | bytes 1179656 | tf_op jit(solution)/shard_map/ppermute | solution.py:46
  30.1 3.6 %collective-permute-done.1.refs_1_ = bf16[12,2,64,128]{3,2,1,0:T(8,128)(2,1)} collective-permute-done((bf16[12,2,64,128]{3,2,1,0:T(8,128)(2,1)S(1)}, bf16[12,2,64,128]{3,2,1,0:T(8,128)(2,1)}, u32[]{:S(2)}, u32[]{:S(2)}) %collective-permute-start.1) | collective-permute-done | bytes 393248 | tf_op jit(solution)/shard_map/ppermute | solution.py:44
  33.7 3.7 %collective-permute-start.5 = (bf16[12,2,64,128]{3,2,1,0:T(8,128)(2,1)}, bf16[12,2,64,128]{3,2,1,0:T(8,128)(2,1)S(1)}, u32[]{:S(2)}, u32[]{:S(2)}) collective-permute-start(bf16[12,2,64,128]{3,2,1,0:T(8,128)(2,1)} %collective-permute-done.1.refs_1_), channel_id=1, source_target_pairs={{0,4},{4,8},{6,2},{8,12},{10,6},{12,16},{14,10},{16,20},{18,14},{2... | collective-permute-start | bytes 1179656 | tf_op jit(solution)/shard_map/ppermute | solution.py:46
  37.6 13.4 %all_to_all.35.codes = s32[16,8,128]{2,1,0:T(8,128)S(1)} all-to-all(s32[16,8,128]{2,1,0:T(8,128)S(1)} %pad.4), channel_id=1, replica_groups=mesh['region'=16,'member'=2] {'region'}, dimensions={0} | all-to-all | bytes 131072 | tf_op jit(solution)/shard_map/all_to_all | solution.py:646
  52.1 3.2 %shard_map.100 = (f32[2,64,128]{2,1,0:T(8,128)S(1)}, bf16[40,64,128]{2,1,0:T(8,128)(2,1)S(1)}, bf16[128,384]{1,0:T(8,128)(2,1)S(1)}, bf16[256,256]{1,0:T(8,128)(2,1)S(1)}, bf16[256,256]{1,0:T(8,128)(2,1)S(1)}) custom-call(s32[16,3]{1,0:T(8,128)S(1)} %copy.14.pattern, f32[40,64,128]{2,1,0:T(8,128)S(1)} %copy-done.2, bf16[40,2,64,128]{3,2,1,0:T(8,128)(2,1)S(1)} %copy-done.1, ...), custom_call_target="tpu_custom_call" | custom-call | tf_op jit(solution)/shard_map/pallas_call | solution.py:52
  55.3 1.8 %shard_map.103 = (bf16[512,1024]{1,0:T(8,128)(2,1)S(1)}, bf16[512,1024]{1,0:T(8,128)(2,1)S(1)}, bf16[3,512,512]{2,1,0:T(8,128)(2,1)S(1)}, bf16[3,256,1024]{2,1,0...) custom-call(s32[8,512]{1,0:T(8,128)S(1)} %broadcast_in_dim.10.position, ...), custom_call_target="tpu_custom_call" | custom-call | tf_op jit(solution)/shard_map/pallas_call | solution.py:52
  57.1 1.8 %shard_map.101 = (f32[2,64,128]{2,1,0:T(8,128)S(1)}, bf16[40,2,64,128]{3,2,1,0:T(8,128)(2,1)S(1)}) custom-call(bf16[8,2,64,128]{3,2,1,0:T(8,128)(2,1)} %collective-permute-done.refs_0_, bf16[12,2,64,128]{3,2,1,0:T(8,128)(2,1)} %collective-permute-done.1.refs_1_, bf16[12,2,64,128]{3,2,1,0:T(8,128)(2,1)} %collective-permute-done.2.refs_2_, ...), custom_call_target="tpu_custom_call" | custom-call | tf_op jit(solution)/shard_map/pallas_call | solution.py:52
  63.5 15.8 %all_to_all.36.recv = bf16[16,96,128]{2,1,0:T(8,128)(2,1)S(1)} all-to-all(bf16[16,96,128]{2,1,0:T(8,128)(2,1)S(1)} %shard_map.105), channel_id=1, replica_groups=mesh['region'=16,'member'=2] {'region'}, dimensions={0} | all-to-all | bytes 786432 | tf_op jit(solution)/shard_map/all_to_all | solution.py:646
  79.3 1.8 shard_map.106
  81.1 15.4 %all_to_all.37.recv = bf16[16,96,128]{2,1,0:T(8,128)(2,1)S(1)} all-to-all(bf16[16,96,128]{2,1,0:T(8,128)(2,1)S(1)} %get-tuple-element.64), channel_id=1, replica_groups=mesh['region'=16,'member'=2] {'region'}, dimensions={0} | all-to-all | bytes 786432 | tf_op jit(solution)/shard_map/all_to_all | solution.py:646
  98.5 4.1 %shard_map.108 = (f32[40,64,128]{2,1,0:T(8,128)S(1)}, f32[3,2,64,128]{3,2,1,0:T(8,128)S(1)}, bf16[3,2,64,128]{3,2,1,0:T(8,128)(2,1)S(1)}, f32[8,128]{1,0:T(8,128)S(1)}) custom-call(bf16[40,2,64,128]{3,2,1,0:T(8,128)(2,1)S(1)} %get-tuple-element.48.refs_0_, bf16[40,2,64,128]{3,2,1,0:T(8,128)(2,1)S(1)} %get-tuple-element.56.refs_1_, ...), custom_call_target="tpu_custom_call" | custom-call | tf_op jit(solution)/shard_map/pallas_call | solution.py:52
  104.6 16.3 %all_to_all.38.recv = bf16[16,96,128]{2,1,0:T(8,128)(2,1)S(1)} all-to-all(bf16[16,96,128]{2,1,0:T(8,128)(2,1)S(1)} %shard_map.109), channel_id=1, replica_groups=mesh['region'=16,'member'=2] {'region'}, dimensions={0} | all-to-all | bytes 786432 | tf_op jit(solution)/shard_map/all_to_all | solution.py:646
  120.9 1.6 shard_map.110
  122.5 15.5 %all_to_all.39.recv = bf16[16,96,128]{2,1,0:T(8,128)(2,1)S(1)} all-to-all(bf16[16,96,128]{2,1,0:T(8,128)(2,1)S(1)} %get-tuple-element.72), channel_id=1, replica_groups=mesh['region'=16,'member'=2] {'region'}, dimensions={0} | all-to-all | bytes 786432 | tf_op jit(solution)/shard_map/all_to_all | solution.py:646
  140.0 4.4 %shard_map.112 = (f32[40,64,128]{2,1,0:T(8,128)S(1)}, f32[3,2,64,128]{3,2,1,0:T(8,128)S(1)}, bf16[3,2,64,128]{3,2,1,0:T(8,128)(2,1)S(1)}, f32[8,128]{1,0:T(8,128)}) custom-call(bf16[40,2,64,128]{3,2,1,0:T(8,128)(2,1)S(1)} %get-tuple-element.48.refs_0_, bf16[40,2,64,128]{3,2,1,0:T(8,128)(2,1)S(1)} %get-tuple-element.56.refs_1_, ...), custom_call_target="tpu_custom_call" | custom-call | tf_op jit(solution)/shard_map/pallas_call | solution.py:52
  146.6 17.0 %all_to_all.40.recv = bf16[16,104,128]{2,1,0:T(8,128)(2,1)S(1)} all-to-all(bf16[16,104,128]{2,1,0:T(8,128)(2,1)S(1)} %shard_map.113), channel_id=1, replica_groups=mesh['region'=16,'member'=2] {'region'}, dimensions={0} | all-to-all | bytes 851968 | tf_op jit(solution)/shard_map/all_to_all | solution.py:646
  165.1 11.0 %all_to_all.41.sums = f32[16,8,128]{2,1,0:T(8,128)S(1)} all-to-all(f32[16,8,128]{2,1,0:T(8,128)S(1)} %get-tuple-element.83), channel_id=1, replica_groups=mesh['region'=16,'member'=2] {'region'}, dimensions={0} | all-to-all | bytes 131072 | tf_op jit(solution)/shard_map/all_to_all | solution.py:646
  (74 shorter events, 22.9 us)
Async XLA Ops:
  0.0 9.9 %copy-start = (s32[1024,1]{0,1:T(1,128)S(1)}, s32[1024,1]{0,1:T(1,128)}, u32[]{:S(2)}) copy-start(s32[1024,1]{0,1:T(1,128)} %param.15) | copy-start | bytes 12292
  1.7 8.5 %copy-start.7 = (s32[1024]{0:T(1024)S(1)}, s32[1024]{0:T(1024)}, u32[]{:S(2)}) copy-start(s32[1024]{0:T(1024)} %param.17) | copy-start | bytes 12292
  1.7 8.5 %copy-start.8 = (s32[1024]{0:T(1024)S(1)}, s32[1024]{0:T(1024)}, u32[]{:S(2)}) copy-start(s32[1024]{0:T(1024)} %param.16) | copy-start | bytes 12292
  1.7 10.4 %collective-permute-start = (bf16[8,2,64,128]{3,2,1,0:T(8,128)(2,1)}, bf16[8,2,64,128]{3,2,1,0:T(8,128)(2,1)}, u32[]{:S(2)}, u32[]{:S(2)}) collective-permute-start(bf16[8,2,64,128]{3,2,1,0:T(8,128)(2,1)} %slice.15), channel_id=1, source_target_pairs={{0,2},{2,0},{4,6},{6,4},{8,10},{10,8},{12,14},{14,12},{16,18},{18,... | collective-permute-start | bytes 786440 | tf_op jit(solution)/shard_map/ppermute | solution.py:44
  6.3 44.7 %copy-start.9 = (s32[16,3]{0,1:T(4,128)S(1)}, s32[16,3]{0,1:T(4,128)}, u32[]{:S(2)}) copy-start(s32[16,3]{0,1:T(4,128)} %param.14) | copy-start | bytes 580
  6.3 44.8 %copy-start.1 = (bf16[40,2,64,128]{3,2,1,0:T(8,128)(2,1)S(1)}, bf16[40,2,64,128]{3,2,1,0:T(8,128)(2,1)}, u32[]{:S(2)}) copy-start(bf16[40,2,64,128]{3,2,1,0:T(8,128)(2,1)} %refs_5_.3) | copy-start | bytes 3932164
  6.3 44.8 %copy-start.2 = (f32[40,64,128]{2,1,0:T(8,128)S(1)}, f32[40,64,128]{2,1,0:T(8,128)}, u32[]{:S(2)}) copy-start(f32[40,64,128]{2,1,0:T(8,128)} %control.1) | copy-start | bytes 3932164
  6.3 44.8 %copy-start.6 = (bf16[64,64]{1,0:T(8,128)(2,1)S(1)}, bf16[64,64]{1,0:T(8,128)(2,1)}, u32[]{:S(2)}) copy-start(bf16[64,64]{1,0:T(8,128)(2,1)} %vloc.1) | copy-start | bytes 24580
  6.3 11.4 %collective-permute-start.3 = (bf16[8,2,64,128]{3,2,1,0:T(8,128)(2,1)}, bf16[8,2,64,128]{3,2,1,0:T(8,128)(2,1)}, u32[]{:S(2)}, u32[]{:S(2)}) collective-permute-start(bf16[8,2,64,128]{3,2,1,0:T(8,128)(2,1)} %slice.22), channel_id=1, source_target_pairs={{0,2},{2,0},{4,6},{6,4},{8,10},{10,8},{12,14},{14,12},{16,18},{18,... | collective-permute-start | bytes 786440 | tf_op jit(solution)/shard_map/ppermute | solution.py:44
  7.8 18.4 %collective-permute-start.2 = (bf16[12,2,64,128]{3,2,1,0:T(8,128)(2,1)S(1)}, bf16[12,2,64,128]{3,2,1,0:T(8,128)(2,1)}, u32[]{:S(2)}, u32[]{:S(2)}) collective-permute-start(bf16[12,2,64,128]{3,2,1,0:T(8,128)(2,1)S(1)} %get-tuple-element.85), channel_id=1, source_target_pairs={{0,2},{2,0},{4,6},{6,4},{8,10},{10,8},{12,14},{14,12},{16,18},{18,... | collective-permute-start | bytes 1179656 | tf_op jit(solution)/shard_map/ppermute | solution.py:44
  9.7 24.1 %collective-permute-start.1 = (bf16[12,2,64,128]{3,2,1,0:T(8,128)(2,1)S(1)}, bf16[12,2,64,128]{3,2,1,0:T(8,128)(2,1)}, u32[]{:S(2)}, u32[]{:S(2)}) collective-permute-start(bf16[12,2,64,128]{3,2,1,0:T(8,128)(2,1)S(1)} %get-tuple-element.86), channel_id=1, source_target_pairs={{0,2},{2,0},{4,6},{6,4},{8,10},{10,8},{12,14},{14,12},{16,18},{18,... | collective-permute-start | bytes 1179656 | tf_op jit(solution)/shard_map/ppermute | solution.py:44
  12.1 46.8 %collective-permute-start.4 = (bf16[8,2,64,128]{3,2,1,0:T(8,128)(2,1)}, bf16[8,2,64,128]{3,2,1,0:T(8,128)(2,1)}, u32[]{:S(2)}, u32[]{:S(2)}) collective-permute-start(bf16[8,2,64,128]{3,2,1,0:T(8,128)(2,1)} %collective-permute-done.refs_0_), channel_id=1, source_target_pairs={{0,4},{4,8},{6,2},{8,12},{10,6},{12,16},{14,10},{16,20},{18,14},{2... | collective-permute-start | bytes 786440 | tf_op jit(solution)/shard_map/ppermute | solution.py:46
  17.7 41.2 %collective-permute-start.7 = (bf16[8,2,64,128]{3,2,1,0:T(8,128)(2,1)}, bf16[8,2,64,128]{3,2,1,0:T(8,128)(2,1)}, u32[]{:S(2)}, u32[]{:S(2)}) collective-permute-start(bf16[8,2,64,128]{3,2,1,0:T(8,128)(2,1)} %collective-permute-done.3.refs_3_), channel_id=1, source_target_pairs={{0,4},{4,8},{6,2},{8,12},{10,6},{12,16},{14,10},{16,20},{18,14},{2... | collective-permute-start | bytes 786440 | tf_op jit(solution)/shard_map/ppermute | solution.py:46
  26.2 32.8 %collective-permute-start.6 = (bf16[12,2,64,128]{3,2,1,0:T(8,128)(2,1)}, bf16[12,2,64,128]{3,2,1,0:T(8,128)(2,1)S(1)}, u32[]{:S(2)}, u32[]{:S(2)}) collective-permute-start(bf16[12,2,64,128]{3,2,1,0:T(8,128)(2,1)} %collective-permute-done.2.refs_2_), channel_id=1, source_target_pairs={{0,4},{4,8},{6,2},{8,12},{10,6},{12,16},{14,10},{16,20},{18,14},{2... | collective-permute-start | bytes 1179656 | tf_op jit(solution)/shard_map/ppermute | solution.py:46
  33.7 25.2 %collective-permute-start.5 = (bf16[12,2,64,128]{3,2,1,0:T(8,128)(2,1)}, bf16[12,2,64,128]{3,2,1,0:T(8,128)(2,1)S(1)}, u32[]{:S(2)}, u32[]{:S(2)}) collective-permute-start(bf16[12,2,64,128]{3,2,1,0:T(8,128)(2,1)} %collective-permute-done.1.refs_1_), channel_id=1, source_target_pairs={{0,4},{4,8},{6,2},{8,12},{10,6},{12,16},{14,10},{16,20},{18,14},{2... | collective-permute-start | bytes 1179656 | tf_op jit(solution)/shard_map/ppermute | solution.py:46
  52.0 3.2 %copy-start.4 = (f32[64,1024]{1,0:T(8,128)S(1)}, f32[64,1024]{1,0:T(8,128)}, u32[]{:S(2)}) copy-start(f32[64,1024]{1,0:T(8,128)} %innov.1) | copy-start | bytes 786436
  61.6 1.4 collective-permute-start.8
  97.1 1.4 collective-permute-start.9
  102.7 1.4 collective-permute-start.10
  138.6 1.4 collective-permute-start.11
  144.3 1.7 collective-permute-start.12
  144.5 1.2 collective-permute-start.13
  144.9 1.2 collective-permute-start.14
  176.1 1.3 collective-permute-start.15
  (2 other events, 4.1 us)

commit v2 on v1

--- a/solution.py
+++ b/solution.py
@@ -14,7 +14,7 @@
 CODES = SLOTS * CELLS
 F32 = jnp.float32
 BF16 = jnp.bfloat16
-HALO_SHARES = (2, 3, 3, 2)
+HALO_SHARES = (3, 3, 2, 2)
 
 
 def near_of(r):
@@ -77,30 +77,28 @@
 
 
 def block_diagonal(matrix, copies, transposed):
-    size = matrix.shape[0]
-    total = copies * size
-    row = lax.broadcasted_iota(jnp.int32, (total, size), 0)
-    place = (row % size == lax.broadcasted_iota(jnp.int32, (total, size), 1)).astype(BF16)
-    tall = dot(place, matrix, ((1,), (1 if transposed else 0,))).astype(BF16)
-    wide = dot(tall, place, ((1,), (1,)))
-    same = (
-        lax.broadcasted_iota(jnp.int32, (total, total), 0) // size
-        == lax.broadcasted_iota(jnp.int32, (total, total), 1) // size
-    )
-    return jnp.where(same, wide, 0.0).astype(BF16)
-
-
-def own_kernel(group, pattern, start, pert, kernels, vloc, inc, lifted, tables, vert, vert_t, acc):
+    side_by_side = jnp.concatenate([matrix] * copies, axis=0)
+    size, total = matrix.shape[0], copies * matrix.shape[0]
+    index = lax.broadcasted_iota(jnp.int32, (size, total), 0)
+    lane = lax.broadcasted_iota(jnp.int32, (size, total), 1)
+    parts = []
+    for i in range(copies):
+        place = (lane == index + i * size).astype(BF16)
+        part = side_by_side[i * size : (i + 1) * size]
+        parts.append(dot(part, place, ((0 if transposed else 1,), (0,))).astype(BF16))
+    return jnp.concatenate(parts, axis=0)
+
+
+def own_kernel(group, pattern, start, pert, kernels, vloc, inc, lifted, tables, vert, vert_t):
     count, lev, _ = start.shape
     rows = group * lev
-    acc[...] = jnp.zeros_like(acc)
     vert[...] = block_diagonal(vloc[...], group, False)
     vert_t[...] = block_diagonal(vloc[...], group, True)
     region = lax.axis_index("region")
     even = region % 2 == 0
-    up = pattern[jnp.minimum(region + 1, pattern.shape[0] - 1), 0]
-    down = pattern[jnp.maximum(region - 1, 0), 2]
-    picks = (pattern[region, 1], jnp.where(even, up, down), jnp.where(even, down, up))
+    up = pattern[0, jnp.minimum(region + 1, pattern.shape[1] - 1)]
+    down = pattern[2, jnp.maximum(region - 1, 0)]
+    picks = (pattern[1, region], jnp.where(even, up, down), jnp.where(even, down, up))
     for t in range(3):
         tables[:, t * CELLS : (t + 1) * CELLS] = kernels[picks[t]]
 
@@ -114,21 +112,18 @@
         local = dot(lifted[at].reshape(rows, CELLS), tables[:, :CELLS])
         values = pert[at]
         for s in range(SLOTS):
-            total = acc[s]
             for j in range(group):
-                total += values[j, s].astype(F32) * local[j * lev : (j + 1) * lev]
-            acc[s] = total
-
-    def step(g, _):
+                totals[s] = totals[s] + values[j, s].astype(F32) * local[j * lev : (j + 1) * lev]
+
+    steps = count // group
+    totals = [jnp.zeros((lev, CELLS), F32)] * SLOTS
+    mix(0)
+    for g in range(1, steps):
+        mix(g)
         gather(g - 1)
-        mix(g)
-        return 0
-
-    steps = count // group
-    mix(0)
-    lax.fori_loop(1, steps, step, 0, unroll=3 if steps % 3 == 1 else 1)
     gather(steps - 1)
-    inc[...] = acc[...]
+    for s in range(SLOTS):
+        inc[s] = totals[s]
 
 
 def own_forward(pattern, start, pert, kernels, vloc, group):
@@ -140,7 +135,6 @@
         functools.partial(own_kernel, group),
         out,
         [start, pert, kernels, vloc],
-        [pltpu.VMEM(field, F32)],
         scalars=[pattern],
     )
 
@@ -148,23 +142,19 @@
 def part_sum(first, group, t, chunks, lifted, tables, acc, full):
     lev = lifted.shape[1]
     rows = group * lev
+    totals = [acc[s] for s in range(SLOTS)]
     for chunk in chunks:
-        size = chunk.shape[0]
-
-        def step(g, _, chunk=chunk, first=first):
-            at = pl.ds(first + g * group, group)
+        for g in range(chunk.shape[0] // group):
+            at = slice(first + g * group, first + (g + 1) * group)
             local = dot(lifted[at].reshape(rows, CELLS), tables[:, t * CELLS : (t + 1) * CELLS])
-            values = chunk[pl.ds(g * group, group)]
+            values = chunk[g * group : (g + 1) * group]
             full[at] = values
             for s in range(SLOTS):
-                total = acc[s]
                 for j in range(group):
-                    total += values[j, s].astype(F32) * local[j * lev : (j + 1) * lev]
-                acc[s] = total
-            return 0
-
-        lax.fori_loop(0, size // group, step, 0, unroll=size // group)
-        first += size
+                    totals[s] = totals[s] + values[j, s].astype(F32) * local[j * lev : (j + 1) * lev]
+        first += chunk.shape[0]
+    for s in range(SLOTS):
+        acc[s] = totals[s]
 
 
 def begin_kernel(n, group, t, *refs):
@@ -299,7 +289,8 @@
         if sign < 0:
             new = -new
         vec[at] = new.reshape(group, lev, CELLS)
-        square[...] += jnp.sum((new * new).reshape(rows // 8, 8, CELLS), axis=0)
+        if sign < 0:
+            square[...] += jnp.sum((new * new).reshape(rows // 8, 8, CELLS), axis=0)
 
     def mix(g):
         half = vec[pl.ds(g * group, group)].reshape(rows, CELLS).astype(BF16)
@@ -706,10 +697,10 @@
     pick, pick_t, onehot, onehot_t, tiles, innov = select_all(
         rows, spots, got_codes, obs_weight, innovations
     )
-    pick, far_p[-1] = lax.optimization_barrier((pick, far_p[-1]))
+    pick, far_p[-2] = lax.optimization_barrier((pick, far_p[-2]))
 
     own, lifted, tables, vert, vert_t = own_forward(
-        loc_pattern, control, perturbations, block_kernels, vertical_loc, group
+        loc_pattern.T, control, perturbations, block_kernels, vertical_loc, group
     )
     near, near_p = begin_part(near_p, 1, lifted, tables, group)
     begun, joined = begin_part(far_p[:-1], 2, lifted, tables, group)

time: 179 us -> 192 us (1.073)
  waiting for transfers between devices: 17 us -> 26 us
  local copies, waits for them, and re-layouts: 5.83 us -> 8.99 us
  blocking collectives: 104 us -> 106 us
    ppermute x4, waiting for transfers between devices: 9.71 us -> 18.7 us  [halo(): near.append(lax.ppermute(chunk, 'region', pairs))]
  transfers between devices with their start and end apart: 16 -> 16, of which waited for: 11 -> 9; matrix products, arithmetic and copies ran while one was open for 2% -> 5% of each run, Pallas kernels for 4% -> 4%
where the time goes in v2:
time: 192 us; the launch traced here: 191 us
  blocking collectives  106 us (55%)
  waiting for transfers between devices  26 us (14%)
  Pallas kernels  25.8 us (13%)
  starting transfers between devices  21.5 us (11%)
  local copies, waits for them, and re-layouts  8.99 us (5%)
    all_to_all x7, blocking collectives, to_regions(): lax.all_to_all(values, 'region', split_axis=0, concat_axis=0, tiled=True)  106 us
    pallas_call x16, Pallas kernels, call(): pl.pallas_call(kernel, out_shape=out_shape, in_specs=[pl.BlockSpec(memory...  25.8 us
    ppermute x4, waiting for transfers between devices, halo(): near.append(lax.ppermute(chunk, 'region', pairs))  18.7 us
    ppermute x4, starting transfers between devices, halo(): far.append(lax.ppermute(chunk, 'region', onward))  15.2 us
    ppermute x6, waiting for transfers between devices, other_members(): return (own, lax.ppermute(half, 'member', [(0, 1), (1, 0)]))  6.27 us
    ppermute x4, starting transfers between devices, halo(): near.append(lax.ppermute(chunk, 'region', pairs))  5.15 us
  transfers between devices with their start and end apart: 16, of which 9 were waited for; matrix products, arithmetic and copies ran while one was open for 5% of the time, Pallas kernels for 4%

profile of v2, /device:TPU:0, one launch (start us, length us, event | category | flops | bytes accessed | tf_op | source)
XLA Modules:
  0.0 191.2 jit_solution(2859536321352044106)
XLA Ops:
  1.1 3.0 %collective-permute-start = (bf16[12,2,64,128]{3,2,1,0:T(8,128)(2,1)S(1)}, bf16[12,2,64,128]{3,2,1,0:T(8,128)(2,1)}, u32[]{:S(2)}, u32[]{:S(2)}) collective-permute-start(bf16[12,2,64,128]{3,2,1,0:T(8,128)(2,1)S(1)} %slice.15), channel_id=1, source_target_pairs={{0,2},{2,0},{4,6},{6,4},{8,10},{10,8},{12,14},{14,12},{16,18},{18,... | collective-permute-start | bytes 1179656 | tf_op jit(solution)/shard_map/ppermute | solution.py:44
  6.2 2.0 %collective-permute-start.3 = (bf16[8,2,64,128]{3,2,1,0:T(8,128)(2,1)}, bf16[8,2,64,128]{3,2,1,0:T(8,128)(2,1)}, u32[]{:S(2)}, u32[]{:S(2)}) collective-permute-start(bf16[8,2,64,128]{3,2,1,0:T(8,128)(2,1)} %get-tuple-element.85), channel_id=1, source_target_pairs={{0,2},{2,0},{4,6},{6,4},{8,10},{10,8},{12,14},{14,12},{16,18},{18,... | collective-permute-start | bytes 786440 | tf_op jit(solution)/shard_map/ppermute | solution.py:44
  9.7 18.5 %collective-permute-done.3.refs_3_ = bf16[8,2,64,128]{3,2,1,0:T(8,128)(2,1)} collective-permute-done((bf16[8,2,64,128]{3,2,1,0:T(8,128)(2,1)}, bf16[8,2,64,128]{3,2,1,0:T(8,128)(2,1)}, u32[]{:S(2)}, u32[]{:S(2)}) %collective-permute-start.3) | collective-permute-done | bytes 262176 | tf_op jit(solution)/shard_map/ppermute | solution.py:44
  28.3 4.7 %collective-permute-start.7 = (bf16[8,2,64,128]{3,2,1,0:T(8,128)(2,1)}, bf16[8,2,64,128]{3,2,1,0:T(8,128)(2,1)}, u32[]{:S(2)}, u32[]{:S(2)}) collective-permute-start(bf16[8,2,64,128]{3,2,1,0:T(8,128)(2,1)} %collective-permute-done.3.refs_3_), channel_id=1, source_target_pairs={{0,4},{4,8},{6,2},{8,12},{10,6},{12,16},{14,10},{16,20},{18,14},{2... | collective-permute-start | bytes 786440 | tf_op jit(solution)/shard_map/ppermute | solution.py:46
  33.1 4.4 %collective-permute-start.6 = (bf16[8,2,64,128]{3,2,1,0:T(8,128)(2,1)}, bf16[8,2,64,128]{3,2,1,0:T(8,128)(2,1)}, u32[]{:S(2)}, u32[]{:S(2)}) collective-permute-start(bf16[8,2,64,128]{3,2,1,0:T(8,128)(2,1)} %collective-permute-done.2.refs_2_), channel_id=1, source_target_pairs={{0,4},{4,8},{6,2},{8,12},{10,6},{12,16},{14,10},{16,20},{18,14},{2... | collective-permute-start | bytes 786440 | tf_op jit(solution)/shard_map/ppermute | solution.py:46
  37.4 2.8 %collective-permute-start.4 = (bf16[12,2,64,128]{3,2,1,0:T(8,128)(2,1)}, bf16[12,2,64,128]{3,2,1,0:T(8,128)(2,1)S(1)}, u32[]{:S(2)}, u32[]{:S(2)}) collective-permute-start(bf16[12,2,64,128]{3,2,1,0:T(8,128)(2,1)} %collective-permute-done.refs_0_), channel_id=1, source_target_pairs={{0,4},{4,8},{6,2},{8,12},{10,6},{12,16},{14,10},{16,20},{18,14},{2... | collective-permute-start | bytes 1179656 | tf_op jit(solution)/shard_map/ppermute | solution.py:46
  40.2 3.4 %collective-permute-start.5 = (bf16[12,2,64,128]{3,2,1,0:T(8,128)(2,1)}, bf16[12,2,64,128]{3,2,1,0:T(8,128)(2,1)S(1)}, u32[]{:S(2)}, u32[]{:S(2)}) collective-permute-start(bf16[12,2,64,128]{3,2,1,0:T(8,128)(2,1)} %collective-permute-done.1.refs_1_), channel_id=1, source_target_pairs={{0,4},{4,8},{6,2},{8,12},{10,6},{12,16},{14,10},{16,20},{18,14},{2... | collective-permute-start | bytes 1179656 | tf_op jit(solution)/shard_map/ppermute | solution.py:46
  49.7 15.4 %all_to_all.35.codes = s32[16,8,128]{2,1,0:T(8,128)S(1)} all-to-all(s32[16,8,128]{2,1,0:T(8,128)S(1)} %pad.4), channel_id=1, replica_groups=mesh['region'=16,'member'=2] {'region'}, dimensions={0} | all-to-all | bytes 131072 | tf_op jit(solution)/shard_map/all_to_all | solution.py:637
  65.8 2.0 %shard_map.100 = (f32[2,64,128]{2,1,0:T(8,128)S(1)}, bf16[40,64,128]{2,1,0:T(8,128)(2,1)S(1)}, bf16[128,384]{1,0:T(8,128)(2,1)S(1)}, bf16[256,256]{1,0:T(8,128)(2,1)S(1)}, bf16[256,256]{1,0:T(8,128)(2,1)S(1)}) custom-call(s32[3,16]{1,0:T(4,128)S(1)} %bitcast.11, f32[40,64,128]{2,1,0:T(8,128)S(1)} %copy-done.2, bf16[40,2,64,128]{3,2,1,0:T(8,128)(2,1)S(1)} %copy-done.1, ...), custom_call_target="tpu_custom_call" | custom-call | tf_op jit(solution)/shard_map/pallas_call | solution.py:52
  67.8 1.8 shard_map.102
  69.6 1.8 shard_map.101
  71.5 1.4 shard_map.103
  76.0 15.8 %all_to_all.36.recv = bf16[16,96,128]{2,1,0:T(8,128)(2,1)S(1)} all-to-all(bf16[16,96,128]{2,1,0:T(8,128)(2,1)S(1)} %shard_map.105), channel_id=1, replica_groups=mesh['region'=16,'member'=2] {'region'}, dimensions={0} | all-to-all | bytes 786432 | tf_op jit(solution)/shard_map/all_to_all | solution.py:637
  91.8 1.8 shard_map.106
  93.6 15.4 %all_to_all.37.recv = bf16[16,96,128]{2,1,0:T(8,128)(2,1)S(1)} all-to-all(bf16[16,96,128]{2,1,0:T(8,128)(2,1)S(1)} %get-tuple-element.64), channel_id=1, replica_groups=mesh['region'=16,'member'=2] {'region'}, dimensions={0} | all-to-all | bytes 786432 | tf_op jit(solution)/shard_map/all_to_all | solution.py:637
  111.0 4.1 %shard_map.108 = (f32[40,64,128]{2,1,0:T(8,128)S(1)}, f32[3,2,64,128]{3,2,1,0:T(8,128)S(1)}, bf16[3,2,64,128]{3,2,1,0:T(8,128)(2,1)S(1)}, f32[8,128]{1,0:T(8,128)S(1)}) custom-call(bf16[40,2,64,128]{3,2,1,0:T(8,128)(2,1)S(1)} %get-tuple-element.48.refs_0_, bf16[40,2,64,128]{3,2,1,0:T(8,128)(2,1)S(1)} %get-tuple-element.56.refs_1_, ...), custom_call_target="tpu_custom_call" | custom-call | tf_op jit(solution)/shard_map/pallas_call | solution.py:52
  117.1 16.3 %all_to_all.38.recv = bf16[16,96,128]{2,1,0:T(8,128)(2,1)S(1)} all-to-all(bf16[16,96,128]{2,1,0:T(8,128)(2,1)S(1)} %shard_map.109), channel_id=1, replica_groups=mesh['region'=16,'member'=2] {'region'}, dimensions={0} | all-to-all | bytes 786432 | tf_op jit(solution)/shard_map/all_to_all | solution.py:637
  133.4 1.6 shard_map.110
  135.0 15.5 %all_to_all.39.recv = bf16[16,96,128]{2,1,0:T(8,128)(2,1)S(1)} all-to-all(bf16[16,96,128]{2,1,0:T(8,128)(2,1)S(1)} %get-tuple-element.72), channel_id=1, replica_groups=mesh['region'=16,'member'=2] {'region'}, dimensions={0} | all-to-all | bytes 786432 | tf_op jit(solution)/shard_map/all_to_all | solution.py:637
  152.5 4.2 %shard_map.112 = (f32[40,64,128]{2,1,0:T(8,128)S(1)}, f32[3,2,64,128]{3,2,1,0:T(8,128)S(1)}, bf16[3,2,64,128]{3,2,1,0:T(8,128)(2,1)S(1)}, f32[8,128]{1,0:T(8,128)}) custom-call(bf16[40,2,64,128]{3,2,1,0:T(8,128)(2,1)S(1)} %get-tuple-element.48.refs_0_, bf16[40,2,64,128]{3,2,1,0:T(8,128)(2,1)S(1)} %get-tuple-element.56.refs_1_, ...), custom_call_target="tpu_custom_call" | custom-call | tf_op jit(solution)/shard_map/pallas_call | solution.py:52
  158.9 17.0 %all_to_all.40.recv = bf16[16,104,128]{2,1,0:T(8,128)(2,1)S(1)} all-to-all(bf16[16,104,128]{2,1,0:T(8,128)(2,1)S(1)} %shard_map.113), channel_id=1, replica_groups=mesh['region'=16,'member'=2] {'region'}, dimensions={0} | all-to-all | bytes 851968 | tf_op jit(solution)/shard_map/all_to_all | solution.py:637
  175.9 1.5 shard_map.114
  177.4 11.0 %all_to_all.41.sums = f32[16,8,128]{2,1,0:T(8,128)S(1)} all-to-all(f32[16,8,128]{2,1,0:T(8,128)S(1)} %get-tuple-element.83), channel_id=1, replica_groups=mesh['region'=16,'member'=2] {'region'}, dimensions={0} | all-to-all | bytes 131072 | tf_op jit(solution)/shard_map/all_to_all | solution.py:637
  189.7 1.5 shard_map.115
  (73 shorter events, 24.0 us)
Async XLA Ops:
  0.0 8.2 %copy-start = (s32[1024,1]{0,1:T(1,128)S(1)}, s32[1024,1]{0,1:T(1,128)}, u32[]{:S(2)}) copy-start(s32[1024,1]{0,1:T(1,128)} %param.15) | copy-start | bytes 12292
  0.0 5.3 %copy-start.1 = (bf16[40,2,64,128]{3,2,1,0:T(8,128)(2,1)S(1)}, bf16[40,2,64,128]{3,2,1,0:T(8,128)(2,1)}, u32[]{:S(2)}) copy-start(bf16[40,2,64,128]{3,2,1,0:T(8,128)(2,1)} %refs_5_.3) | copy-start | bytes 3932164
  0.0 8.5 %copy-start.9 = (s32[1024]{0:T(1024)S(1)}, s32[1024]{0:T(1024)}, u32[]{:S(2)}) copy-start(s32[1024]{0:T(1024)} %param.17) | copy-start | bytes 12292
  1.1 36.3 %collective-permute-start = (bf16[12,2,64,128]{3,2,1,0:T(8,128)(2,1)S(1)}, bf16[12,2,64,128]{3,2,1,0:T(8,128)(2,1)}, u32[]{:S(2)}, u32[]{:S(2)}) collective-permute-start(bf16[12,2,64,128]{3,2,1,0:T(8,128)(2,1)S(1)} %slice.15), channel_id=1, source_target_pairs={{0,2},{2,0},{4,6},{6,4},{8,10},{10,8},{12,14},{14,12},{16,18},{18,... | collective-permute-start | bytes 1179656 | tf_op jit(solution)/shard_map/ppermute | solution.py:44
  5.2 59.9 %copy-start.2 = (f32[40,64,128]{2,1,0:T(8,128)S(1)}, f32[40,64,128]{2,1,0:T(8,128)}, u32[]{:S(2)}) copy-start(f32[40,64,128]{2,1,0:T(8,128)} %control.1) | copy-start | bytes 3932164
  5.2 59.8 %copy-start.5 = (bf16[4,128,128]{2,1,0:T(8,128)(2,1)S(1)}, bf16[4,128,128]{2,1,0:T(8,128)(2,1)}, u32[]{:S(2)}) copy-start(bf16[4,128,128]{2,1,0:T(8,128)(2,1)} %kernels.1) | copy-start | bytes 393220
  5.2 59.8 %copy-start.7 = (s32[16,3]{0,1:T(4,128)S(1)}, s32[16,3]{0,1:T(4,128)}, u32[]{:S(2)}) copy-start(s32[16,3]{0,1:T(4,128)} %param.14) | copy-start | bytes 580
  5.2 35.0 %collective-permute-start.1 = (bf16[12,2,64,128]{3,2,1,0:T(8,128)(2,1)S(1)}, bf16[12,2,64,128]{3,2,1,0:T(8,128)(2,1)}, u32[]{:S(2)}, u32[]{:S(2)}) collective-permute-start(bf16[12,2,64,128]{3,2,1,0:T(8,128)(2,1)S(1)} %slice.20), channel_id=1, source_target_pairs={{0,2},{2,0},{4,6},{6,4},{8,10},{10,8},{12,14},{14,12},{16,18},{18,... | collective-permute-start | bytes 1179656 | tf_op jit(solution)/shard_map/ppermute | solution.py:44
  6.2 22.1 %collective-permute-start.3 = (bf16[8,2,64,128]{3,2,1,0:T(8,128)(2,1)}, bf16[8,2,64,128]{3,2,1,0:T(8,128)(2,1)}, u32[]{:S(2)}, u32[]{:S(2)}) collective-permute-start(bf16[8,2,64,128]{3,2,1,0:T(8,128)(2,1)} %get-tuple-element.85), channel_id=1, source_target_pairs={{0,2},{2,0},{4,6},{6,4},{8,10},{10,8},{12,14},{14,12},{16,18},{18,... | collective-permute-start | bytes 786440 | tf_op jit(solution)/shard_map/ppermute | solution.py:44
  8.2 24.9 %collective-permute-start.2 = (bf16[8,2,64,128]{3,2,1,0:T(8,128)(2,1)}, bf16[8,2,64,128]{3,2,1,0:T(8,128)(2,1)}, u32[]{:S(2)}, u32[]{:S(2)}) collective-permute-start(bf16[8,2,64,128]{3,2,1,0:T(8,128)(2,1)} %get-tuple-element.86), channel_id=1, source_target_pairs={{0,2},{2,0},{4,6},{6,4},{8,10},{10,8},{12,14},{14,12},{16,18},{18,... | collective-permute-start | bytes 786440 | tf_op jit(solution)/shard_map/ppermute | solution.py:44
  28.3 44.6 %collective-permute-start.7 = (bf16[8,2,64,128]{3,2,1,0:T(8,128)(2,1)}, bf16[8,2,64,128]{3,2,1,0:T(8,128)(2,1)}, u32[]{:S(2)}, u32[]{:S(2)}) collective-permute-start(bf16[8,2,64,128]{3,2,1,0:T(8,128)(2,1)} %collective-permute-done.3.refs_3_), channel_id=1, source_target_pairs={{0,4},{4,8},{6,2},{8,12},{10,6},{12,16},{14,10},{16,20},{18,14},{2... | collective-permute-start | bytes 786440 | tf_op jit(solution)/shard_map/ppermute | solution.py:46
  33.1 38.4 %collective-permute-start.6 = (bf16[8,2,64,128]{3,2,1,0:T(8,128)(2,1)}, bf16[8,2,64,128]{3,2,1,0:T(8,128)(2,1)}, u32[]{:S(2)}, u32[]{:S(2)}) collective-permute-start(bf16[8,2,64,128]{3,2,1,0:T(8,128)(2,1)} %collective-permute-done.2.refs_2_), channel_id=1, source_target_pairs={{0,4},{4,8},{6,2},{8,12},{10,6},{12,16},{14,10},{16,20},{18,14},{2... | collective-permute-start | bytes 786440 | tf_op jit(solution)/shard_map/ppermute | solution.py:46
  37.4 34.0 %collective-permute-start.4 = (bf16[12,2,64,128]{3,2,1,0:T(8,128)(2,1)}, bf16[12,2,64,128]{3,2,1,0:T(8,128)(2,1)S(1)}, u32[]{:S(2)}, u32[]{:S(2)}) collective-permute-start(bf16[12,2,64,128]{3,2,1,0:T(8,128)(2,1)} %collective-permute-done.refs_0_), channel_id=1, source_target_pairs={{0,4},{4,8},{6,2},{8,12},{10,6},{12,16},{14,10},{16,20},{18,14},{2... | collective-permute-start | bytes 1179656 | tf_op jit(solution)/shard_map/ppermute | solution.py:46
  40.2 31.3 %collective-permute-start.5 = (bf16[12,2,64,128]{3,2,1,0:T(8,128)(2,1)}, bf16[12,2,64,128]{3,2,1,0:T(8,128)(2,1)S(1)}, u32[]{:S(2)}, u32[]{:S(2)}) collective-permute-start(bf16[12,2,64,128]{3,2,1,0:T(8,128)(2,1)} %collective-permute-done.1.refs_1_), channel_id=1, source_target_pairs={{0,4},{4,8},{6,2},{8,12},{10,6},{12,16},{14,10},{16,20},{18,14},{2... | collective-permute-start | bytes 1179656 | tf_op jit(solution)/shard_map/ppermute | solution.py:46
  65.8 2.0 %copy-start.3 = (f32[8,128,128]{2,1,0:T(8,128)S(1)}, f32[8,128,128]{2,1,0:T(8,128)}, u32[]{:S(2)}) copy-start(f32[8,128,128]{2,1,0:T(8,128)} %weight.1) | copy-start | bytes 1572868
  65.8 2.0 %copy-start.4 = (f32[64,1024]{1,0:T(8,128)S(1)}, f32[64,1024]{1,0:T(8,128)}, u32[]{:S(2)}) copy-start(f32[64,1024]{1,0:T(8,128)} %innov.1) | copy-start | bytes 786436
  74.1 1.4 collective-permute-start.8
  109.6 1.4 collective-permute-start.9
  115.1 1.4 collective-permute-start.10
  151.1 1.4 collective-permute-start.11
  156.7 1.7 collective-permute-start.12
  156.8 1.2 collective-permute-start.13
  157.2 1.2 collective-permute-start.14
  188.5 1.3 collective-permute-start.15
  (2 other events, 1.3 us)
